TPU v7x, 512 devices: a whole 4x4x16 slice. The times are simulated.
512 devices in a mesh: mp: 8 (over x, z_hi), tok: 64 (over y, z_lo, core).
Axes of the slice: x: 4, y: 4, z: 16 (z_hi: 2, z_lo: 8; z = z_hi * 8 + z_lo), core: 2. Of those that a mesh axis runs over, the one named last changes fastest.
Arguments:
- inputs: bfloat16 [8, 64, 128, 2048], P('mp', 'tok'), may hold values from -6 to 6
- cotangent: bfloat16 [8, 64, 128, 4096], P('mp', 'tok'), may hold values from -6 to 6
- token_ids: int32 [8, 64, 128], P('mp', 'tok'), may hold values from 0 to 151935
- weights: float32 [8, 64, 256, 512], P('mp', 'tok'), may hold values from -6 to 6
Outputs:
- merged: float32 [64, 256, 512], P('tok')
All inputs are finite; a program needn't handle non-finite values.
Results may differ from a plain program's by a relative error of at most 0.0003.
Values may be sent and summed in bfloat16 or wider, within the bound.
A program may use at most 64 MiB of HBM per device.

v0:
```python
import math

import jax
import jax.numpy as jnp
from jax import lax
from jax.sharding import PartitionSpec as P

ROW_BLOCKS = 8
FIRST_TEXT = 37984


damping = 0.1


def squares(operands):
    row_parts, col_parts = operands
    src_count = row_parts.shape[0]
    item_count = row_parts.shape[1]
    seq_length = row_parts.shape[2]
    row_width = row_parts.shape[3]
    col_width = col_parts.shape[3]
    row_parts = row_parts.reshape(src_count // 8, 8, item_count, seq_length, row_width)
    col_parts = col_parts.reshape(src_count // 8, 8, item_count, seq_length, col_width)
    factor = 1.0 / math.sqrt(seq_length)

    def accumulate(summed, couple):
        gradient = (
            jnp.einsum("gitr,gitc->girc", couple[0], couple[1], preferred_element_type=jnp.float32)
            * factor
        )
        return (summed + jnp.sum(gradient * gradient, axis=0), None)

    start = jnp.zeros((item_count, row_width, col_width), jnp.float32)
    summed, unused = lax.scan(accumulate, start, (row_parts, col_parts))
    return summed


def shards(inputs, cotangent, token_ids, weights):
    device_count = lax.axis_size("tok")
    col_count = device_count // ROW_BLOCKS
    seq_count = inputs.shape[1]
    seq_length = inputs.shape[2]
    feature_width = inputs.shape[3]
    query_width = cotangent.shape[3]
    row_width = feature_width // ROW_BLOCKS
    col_width = query_width // col_count
    kept_mask = (token_ids[0] >= FIRST_TEXT).astype(jnp.bfloat16)
    masked = cotangent[0] * kept_mask[:, :, None]
    row_send = inputs[0].reshape(seq_count, seq_length, ROW_BLOCKS, row_width).transpose(2, 0, 1, 3)
    row_send = jnp.repeat(row_send, col_count, axis=0)
    col_send = masked.reshape(seq_count, seq_length, col_count, col_width).transpose(2, 0, 1, 3)
    col_send = jnp.tile(col_send, (ROW_BLOCKS, 1, 1, 1))
    per_item = squares(
        (
            lax.all_to_all(row_send, "tok", split_axis=0, concat_axis=0, tiled=True),
            lax.all_to_all(col_send, "tok", split_axis=0, concat_axis=0, tiled=True),
        )
    )
    fisher = jnp.sum(per_item, axis=0) / (seq_count * device_count)
    damped = fisher + damping
    product = damped * weights[0, 0]
    totals = lax.psum((damped, product), "mp")
    merged = totals[1] / totals[0]
    return merged[None]


def solution(mesh):
    in_specs = (
        P("mp", "tok", None, None),
        P("mp", "tok", None, None),
        P("mp", "tok", None),
        P("mp", "tok", None, None),
    )
    out_specs = P("tok", None, None)
    return jax.shard_map(shards, mesh=mesh, in_specs=in_specs, out_specs=out_specs, check_vma=False)
```

profile of v0, /device:TPU:16, one launch (start us, length us, event | category | flops | bytes accessed | tf_op | source)
XLA Modules:
  0.0 850.2 jit_solution(16942126086965262584)
XLA Ops:
  6.5 1.1 copy.11
  7.7 0.4 copy.7
  8.2 3.0 broadcast_in_dim.13
  11.2 16.5 %all-to-all-start = ((bf16[64,1,128,256]{2,3,1,0:T(8,128)(2,1)}), bf16[64,1,128,256]{2,3,1,0:T(8,128)(2,1)}, u32[]{:S(2)}, u32[]{:S(2)}) async-start(bf16[64,1,128,256]{2,3,1,0:T(8,128)(2,1)} %bitcast.57), calls=%async_computation | async-start | bytes 8388608 | tf_op jit(solution)/shard_map/all_to_all | solution.py:55
  27.7 0.4 copy.12
  28.1 0.2 fusion.5
  28.3 0.3 copy.8
  28.6 181.4 %all-to-all-done = bf16[64,1,128,256]{2,3,1,0:T(8,128)(2,1)} async-done(((bf16[64,1,128,256]{2,3,1,0:T(8,128)(2,1)}), bf16[64,1,128,256]{2,3,1,0:T(8,128)(2,1)}, u32[]{:S(2)}, u32[]{:S(2)}) %all-to-all-start) | async-done | bytes 4194336 | tf_op jit(solution)/shard_map/all_to_all | solution.py:55
  210.0 4.2 tile.12
  214.2 12.1 %all-to-all-start.1 = ((bf16[64,1,128,512]{3,2,1,0:T(8,128)(2,1)}), bf16[64,1,128,512]{3,2,1,0:T(8,128)(2,1)}, u32[]{:S(2)}, u32[]{:S(2)}) async-start(bf16[64,1,128,512]{3,2,1,0:T(8,128)(2,1)} %bitcast.56), calls=%async_computation.1 | async-start | bytes 16777216 | tf_op jit(solution)/shard_map/all_to_all | solution.py:56
  226.4 358.6 %all-to-all-done.1 = bf16[64,1,128,512]{3,2,1,0:T(8,128)(2,1)} async-done(((bf16[64,1,128,512]{3,2,1,0:T(8,128)(2,1)}), bf16[64,1,128,512]{3,2,1,0:T(8,128)(2,1)}, u32[]{:S(2)}, u32[]{:S(2)}) %all-to-all-start.1) | async-done | bytes 8388640 | tf_op jit(solution)/shard_map/all_to_all | solution.py:56
  585.0 18.9 %while.11 = (s32[]{:T(128)}, f32[1,256,512]{2,1,0:T(8,128)S(1)}, bf16[8,8,1,128,256]{3,4,1,2,0:T(8,128)(2,1)}, bf16[8,8,1,128,512]{4,3,1,2,0:T(8,128)(2,1)}, s32[]{:T(128)}, /*index=5*/s32[]{:T(128)}) while((s32[]{:T(128)}, f32[1,256,512]{2,1,0:T(8,128)S(1)}, bf16[8,8,1,128,256]{3,4,1,2,0:T(8,128)(2,1)}, ...), condition=%wide.region_2.3_spmd.clone, body=%wide.region_0.2_spmd.clone.sunk | while | flops 271712256 | bytes 3671119 | solution.py:34
  585.0 2.2 multiply_reduce_fusion.2
  587.4 2.1 multiply_reduce_fusion.2
  589.7 2.1 multiply_reduce_fusion.2
  592.1 2.1 multiply_reduce_fusion.2
  594.5 2.1 multiply_reduce_fusion.2
  596.8 2.1 multiply_reduce_fusion.2
  599.2 2.1 multiply_reduce_fusion.2
  601.5 2.1 multiply_reduce_fusion.2
  603.9 0.9 add_bitcast_fusion
  604.8 0.9 bitcast_multiply_fusion.1
  605.7 235.6 %all-reduce.3.cloned.1.call-done = (f32[256,512]{1,0:T(8,128)}, f32[256,512]{1,0:T(8,128)}) async-done(((f32[256,512]{1,0:T(8,128)}, f32[256,512]{1,0:T(8,128)}), (f32[256,512]{1,0:T(8,128)}, f32[256,512]{1,0:T(8,128)})) %all-reduce.3.cloned.1.call-update) | async-done | bytes 1048592 | tf_op jit(solution)/shard_map/psum | solution.py:62
  841.3 2.1 divide_bitcast_fusion
  (19 shorter events, 1.6 us)
Async XLA Ops:
  11.2 16.5 %copy-start = (bf16[1,1,128,4096]{3,2,1,0:T(8,128)(2,1)S(1)}, bf16[1,1,128,4096]{3,2,1,0:T(8,128)(2,1)}, u32[]{:S(2)}) copy-start(bf16[1,1,128,4096]{3,2,1,0:T(8,128)(2,1)} %param.7) | copy-start | bytes 3145732
  11.2 16.9 %copy-start.2 = (s32[1,1,128]{2,1,0:T(1,128)S(1)}, s32[1,1,128]{2,1,0:T(1,128)}, u32[]{:S(2)}) copy-start(s32[1,1,128]{2,1,0:T(1,128)} %param.8) | copy-start | bytes 1540
  11.2 198.8 %all-to-all-start = ((bf16[64,1,128,256]{2,3,1,0:T(8,128)(2,1)}), bf16[64,1,128,256]{2,3,1,0:T(8,128)(2,1)}, u32[]{:S(2)}, u32[]{:S(2)}) async-start(bf16[64,1,128,256]{2,3,1,0:T(8,128)(2,1)} %bitcast.57), calls=%async_computation | async-start | bytes 8388608 | tf_op jit(solution)/shard_map/all_to_all | solution.py:55
  214.2 370.7 %all-to-all-start.1 = ((bf16[64,1,128,512]{3,2,1,0:T(8,128)(2,1)}), bf16[64,1,128,512]{3,2,1,0:T(8,128)(2,1)}, u32[]{:S(2)}, u32[]{:S(2)}) async-start(bf16[64,1,128,512]{3,2,1,0:T(8,128)(2,1)} %bitcast.56), calls=%async_computation.1 | async-start | bytes 16777216 | tf_op jit(solution)/shard_map/all_to_all | solution.py:56
  226.4 614.9 %all-reduce.3.cloned.1.call-start = ((), (), s32[]{:S(2)}) async-start(), calls=%async_computation.2 | async-start | bytes 2097152 | tf_op jit(solution)/shard_map/psum | solution.py:62
  585.0 19.8 %copy-start.1 = (f32[1,1,256,512]{3,2,1,0:T(8,128)S(1)}, f32[1,1,256,512]{3,2,1,0:T(8,128)}, u32[]{:S(2)}) copy-start(f32[1,1,256,512]{3,2,1,0:T(8,128)} %param.9) | copy-start | bytes 1572868
Sparse Core Ops, SparseCore 0:
  605.8 235.4 all-reduce.2
where the time goes:
time: 851 us; the launch traced here: 850 us
  waiting for transfers between devices  776 us (91%)
  starting transfers between devices  28.6 us (3%)
  matrix products  17.2 us (2%)
  between operations  13.5 us (2%)
  local copies, waits for them, and re-layouts  9.61 us (1%)
    all_to_all x1, waiting for transfers between devices, shards(): lax.all_to_all(col_send, 'tok', split_axis=0, concat_axis=0, tiled=True)  359 us
    psum x1, waiting for transfers between devices, shards(): totals = lax.psum((damped, product), 'mp')  236 us
    all_to_all x1, waiting for transfers between devices, shards(): lax.all_to_all(row_send, 'tok', split_axis=0, concat_axis=0, tiled=True)  181 us
    dot_general x8, matrix products, accumulate(): jnp.einsum('gitr,gitc->girc', couple[0], couple[1], preferred_element_typ...  17.2 us
  transfers between devices with their start and end apart: 3, of which 3 were waited for; matrix products, arithmetic and copies ran while one was open for 0% of the time, Pallas kernels for 0%

commit v1 on v0

v1 whole, which is shorter than its diff:
```python
import jax
import jax.numpy as jnp
from jax import lax
from jax.experimental import pallas as pl
from jax.experimental.pallas import tpu as pltpu
from jax.sharding import PartitionSpec as P

FIRST_TEXT = 37984
DAMPING = 0.1
SUBS = 4
MESH = pl.DeviceIdType.MESH
Y_PEERS = ((1, 0), (3, 0), (1, 1), (3, 1), (2, 0), (2, 1), (0, 1))


def kernel(
    xt_ref, g_ref, w_ref, out_ref,
    rows, cols, fisher, chain, total, parts, wparts, sums, far, merged,
    row_s, row_r, col_s, col_r, chain_s, chain_r,
    w_s, w_r, part_s, part_r, far_s, far_r, out_s, out_r,
):
    mp = lax.axis_index("mp")
    tok = lax.axis_index("tok")
    x, zh = mp // 2, mp % 2
    y, z, c = tok // 16, (tok // 2) % 8, tok % 2
    me = y * 2 + c
    seq = xt_ref.shape[1]
    width = fisher.shape[2]
    height = fisher.shape[1]
    piece = height // SUBS
    band = piece // 4

    def at_y(dy, dc):
        there = (y + dy) % 4
        core = 1 - c if dc else c
        return there, core, (mp, (there * 8 + z) * 2 + core)

    def at_x(dx):
        there = (x + dx) % 4
        return there, (there * 2 + zh, tok)

    def at_z(dz):
        deep = zh * 8 + z + dz + 16
        return (x * 2 + (deep // 8) % 2, (y * 8 + deep % 8) * 2 + c)

    barrier = pltpu.get_barrier_semaphore()
    for dy, dc in Y_PEERS:
        pl.semaphore_signal(barrier, 1, device_id=at_y(dy, dc)[2], device_id_type=MESH)
    for dx in (1, 2, 3):
        pl.semaphore_signal(barrier, 1, device_id=at_x(dx)[1], device_id_type=MESH)
    for dz in (1, -1, 8):
        pl.semaphore_signal(barrier, 1, device_id=at_z(dz), device_id_type=MESH)
    pl.semaphore_wait(barrier, len(Y_PEERS) + 6)

    low = z < 4

    def k_of(i):
        return jnp.where(low, 3 - i, i)

    def row_copy(dy, dc, owner):
        there, core, device = at_y(dy, dc)
        slot = there * 2 + core if owner else me
        return pltpu.make_async_remote_copy(
            src_ref=xt_ref.at[pl.ds(there * 2 * height, 2 * height)],
            dst_ref=rows.at[slot],
            send_sem=row_s.at[there * 2 + core],
            recv_sem=row_r.at[slot],
            device_id=device,
            device_id_type=MESH,
        )

    def col_copy(k, dy, dc, owner):
        there, core, device = at_y(dy, dc)
        slot = there * 2 + core if owner else me
        return pltpu.make_async_remote_copy(
            src_ref=g_ref.at[:, pl.ds(pl.multiple_of((2 * k + core) * width, width), width)],
            dst_ref=cols.at[slot, k],
            send_sem=col_s.at[k, there * 2 + core],
            recv_sem=col_r.at[k, slot],
            device_id=device,
            device_id_type=MESH,
        )

    def w_copy(dx, owner):
        there, device = at_x(dx)
        slot = there if owner else x
        return pltpu.make_async_remote_copy(
            src_ref=w_ref.at[:, there],
            dst_ref=wparts.at[slot],
            send_sem=w_s.at[there],
            recv_sem=w_r.at[slot],
            device_id=device,
            device_id_type=MESH,
        )

    for dy, dc in Y_PEERS:
        row_copy(dy, dc, False).start()

    @pl.loop(0, 4)
    def _(i):
        for dy, dc in Y_PEERS:
            col_copy(k_of(i), dy, dc, False).start()

    for dx in (1, 2, 3):
        w_copy(dx, False).start()

    rows[me] = xt_ref[pl.ds(y * 2 * height, 2 * height), :]
    for k in range(4):
        cols[me, k] = g_ref[:, pl.ds(pl.multiple_of((2 * k + c) * width, width), width)]
    wparts[x] = w_ref[:, x]

    fisher[...] = jnp.zeros_like(fisher)

    for dy, dc in Y_PEERS:
        row_copy(dy, dc, True).wait_recv()

    def compute(i):
        k = k_of(i)
        for dy, dc in Y_PEERS:
            col_copy(k, dy, dc, True).wait_recv()

        @pl.loop(0, 8)
        def _(slot):
            right = cols[slot, k]
            for h in range(2):
                left = rows[slot, h * height:(h + 1) * height, :]
                gradient = jnp.dot(left, right, preferred_element_type=jnp.float32)
                fisher[4 * h + k] += gradient * gradient

    def chain_copy(way, d, s, source):
        span = pl.ds(s * piece, piece)
        return pltpu.make_async_remote_copy(
            src_ref=source.at[span],
            dst_ref=chain.at[way, d, span],
            send_sem=chain_s.at[way, d, s],
            recv_sem=chain_r.at[way, d, s],
            device_id=at_z(1 - 2 * way),
            device_id_type=MESH,
        )

    def chain_step(way, d):
        ahead = (d - z) * (1 - 2 * way)
        first = z == 7 * way

        @pl.when(jnp.logical_and(first, ahead > 0))
        def _():
            for s in range(SUBS):
                chain_copy(way, d, s, fisher.at[d]).start()

        @pl.when(jnp.logical_and(jnp.logical_not(first), ahead > 0))
        def _():
            for s in range(SUBS):
                span = slice(s * piece, (s + 1) * piece)
                chain_copy(way, d, s, chain.at[way, d]).wait_recv()
                chain[way, d, span] += fisher[d, span]
                chain_copy(way, d, s, chain.at[way, d]).start()

    main = jnp.where(low, 0, 1)
    place = jnp.where(low, z, 7 - z)

    def flip(d):
        return jnp.where(low, d, 7 - d)

    for i in range(4):
        compute(i)

        @pl.when(place == 0)
        def _():
            chain_step(main, flip(7 - i))

        if i > 0:
            @pl.when(place > 0)
            def _():
                chain_step(main, flip(8 - i))

    @pl.when(place > 0)
    def _():
        chain_step(main, flip(4))

    for i in range(3):
        chain_step(1 - main, flip(i))
        chain_step(main, flip(3 - i))

    def part_copy(s, dx, owner):
        there, device = at_x(dx)
        slot = there if owner else x
        return pltpu.make_async_remote_copy(
            src_ref=total.at[s, there],
            dst_ref=parts.at[s, slot],
            send_sem=part_s.at[s, there],
            recv_sem=part_r.at[s, slot],
            device_id=device,
            device_id_type=MESH,
        )

    def far_copy(s):
        return pltpu.make_async_remote_copy(
            src_ref=sums.at[s],
            dst_ref=far.at[s],
            send_sem=far_s.at[s],
            recv_sem=far_r.at[s],
            device_id=at_z(8),
            device_id_type=MESH,
        )

    def out_copy(s, dx, owner):
        there, device = at_x(dx)
        slot = there if owner else x
        return pltpu.make_async_remote_copy(
            src_ref=merged.at[s, slot],
            dst_ref=merged.at[s, slot],
            send_sem=out_s.at[s, there],
            recv_sem=out_r.at[s, slot],
            device_id=device,
            device_id_type=MESH,
        )

    scale = 1.0 / (seq * 64)
    for s in range(SUBS):
        span = slice(s * piece, (s + 1) * piece)
        for q in range(4):
            total[s, q] = fisher[z, s * piece + q * band:s * piece + (q + 1) * band]
        for way in (0, 1):
            @pl.when(z != 7 * way)
            def _():
                chain_copy(way, z, s, chain.at[way, z]).wait_recv()
                for q in range(4):
                    total[s, q] += chain[way, z, s * piece + q * band:s * piece + (q + 1) * band]
        for dx in (1, 2, 3):
            part_copy(s, dx, False).start()
        parts[s, x] = total[s, x]

    for dx in (1, 2, 3):
        w_copy(dx, True).wait_recv()
    for s in range(SUBS):
        for dx in (1, 2, 3):
            part_copy(s, dx, True).wait_recv()
        damped = [parts[s, m] * scale + DAMPING for m in range(4)]
        product = [damped[m] * wparts[m, s] for m in range(4)]
        sums[s, 0] = (product[0] + product[1]) + (product[2] + product[3])
        sums[s, 1] = (damped[0] + damped[1]) + (damped[2] + damped[3])
        far_copy(s).start()
    for s in range(SUBS):
        far_copy(s).wait_recv()
        merged[s, x] = (sums[s, 0] + far[s, 0]) / (sums[s, 1] + far[s, 1])
        for dx in (1, 2, 3):
            out_copy(s, dx, False).start()
    for s in range(SUBS):
        for dx in (1, 2, 3):
            out_copy(s, dx, True).wait_recv()
    out_ref[...] = merged[...]

    for dy, dc in Y_PEERS:
        row_copy(dy, dc, False).wait_send()

    @pl.loop(0, 4)
    def _(k):
        for dy, dc in Y_PEERS:
            col_copy(k, dy, dc, False).wait_send()

    for dx in (1, 2, 3):
        w_copy(dx, False).wait_send()
        for s in range(SUBS):
            part_copy(s, dx, False).wait_send()
            out_copy(s, dx, False).wait_send()
    for s in range(SUBS):
        far_copy(s).wait_send()

    @pl.loop(0, 8)
    def _(d):
        for way in (0, 1):
            @pl.when((d - z) * (1 - 2 * way) > 0)
            def _():
                for s in range(SUBS):
                    chain_copy(way, d, s, fisher.at[d]).wait_send()


def shards(inputs, cotangent, token_ids, weights):
    seq, feature = inputs.shape[2:]
    query = cotangent.shape[3]
    height, width = weights.shape[2:]
    band = height // SUBS // 4
    kept = (token_ids[0, 0] >= FIRST_TEXT).astype(jnp.bfloat16)
    turned = (inputs[0, 0] * kept[:, None]).T
    blocks = weights[0, 0].reshape(SUBS, 4, band, width)
    vmem = pl.BlockSpec(memory_space=pltpu.VMEM)
    dma = pltpu.SemaphoreType.DMA
    merged = pl.pallas_call(
        kernel,
        out_shape=jax.ShapeDtypeStruct((SUBS, 4, band, width), jnp.float32),
        in_specs=[vmem] * 3,
        out_specs=vmem,
        scratch_shapes=[
            pltpu.VMEM((8, 2 * height, seq), jnp.bfloat16),
            pltpu.VMEM((8, 4, seq, width), jnp.bfloat16),
            pltpu.VMEM((8, height, width), jnp.float32),
            pltpu.VMEM((2, 8, height, width), jnp.float32),
            pltpu.VMEM((SUBS, 4, band, width), jnp.float32),
            pltpu.VMEM((SUBS, 4, band, width), jnp.float32),
            pltpu.VMEM((4, SUBS, band, width), jnp.float32),
            pltpu.VMEM((SUBS, 2, band, width), jnp.float32),
            pltpu.VMEM((SUBS, 2, band, width), jnp.float32),
            pltpu.VMEM((SUBS, 4, band, width), jnp.float32),
            dma((8,)), dma((8,)), dma((4, 8)), dma((4, 8)),
            dma((2, 8, SUBS)), dma((2, 8, SUBS)),
            dma((4,)), dma((4,)), dma((SUBS, 4)), dma((SUBS, 4)),
            dma((SUBS,)), dma((SUBS,)), dma((SUBS, 4)), dma((SUBS, 4)),
        ],
        compiler_params=pltpu.CompilerParams(
            collective_id=0, has_side_effects=True, vmem_limit_bytes=48 * 1024 * 1024
        ),
    )(turned, cotangent[0, 0], blocks)
    return merged.reshape(1, height, width)


def solution(mesh):
    in_specs = (
        P("mp", "tok", None, None),
        P("mp", "tok", None, None),
        P("mp", "tok", None),
        P("mp", "tok", None, None),
    )
    out_specs = P("tok", None, None)
    return jax.shard_map(shards, mesh=mesh, in_specs=in_specs, out_specs=out_specs, check_vma=False)
```

time: 851 us -> 185 us (0.22)
  the two profiles are of different devices: /device:TPU:16 before, /device:TPU:64 now
where the time goes in v1:
time: 185 us
  Pallas kernels  181 us (98%)
  local copies, waits for them, and re-layouts  3.83 us (2%)
    pallas_call x1, Pallas kernels, shards(): pl.pallas_call(kernel, out_shape=jax.ShapeDtypeStruct((SUBS, 4, band, wid...  181 us
    unnamed x8, local copies, waits for them, and re-layouts  3.83 us

profile of v1, /device:TPU:64, one launch (start us, length us, event | category | flops | bytes accessed | tf_op | source)
XLA Modules:
  0.0 185.2 jit_solution(6848469967168141641)
XLA Ops:
  0.0 0.0 copy-start.2
  0.0 0.7 copy-done.2
  0.7 0.0 copy-start
  0.7 1.4 copy.5
  2.1 0.0 copy-start.1
  2.1 0.0 copy-done
  2.1 1.0 copy-done.1
  3.1 181.3 %shard_map.46 = f32[4,4,16,512]{3,2,1,0:T(8,128)S(1)} custom-call(bf16[2048,128]{1,0:T(8,128)(2,1)S(1)} %fusion.xt_ref, bf16[128,4096]{1,0:T(8,128)(2,1)S(1)} %bitcast.12, f32[4,4,16,512]{3,2,1,0:T(8,128)S(1)} %bitcast.13), custom_call_target="tpu_custom_call" | custom-call | tf_op jit(solution)/shard_map/pallas_call | solution.py:287
  184.4 0.8 copy.7
  (2 shorter events, 0.0 us)
Async XLA Ops:
  0.0 0.7 copy-start.2
  0.7 1.5 copy-start
  2.1 1.0 copy-start.1

commit v2 on v1

--- a/solution.py
+++ b/solution.py
@@ -10,12 +10,27 @@
 SUBS = 4
 MESH = pl.DeviceIdType.MESH
 Y_PEERS = ((1, 0), (3, 0), (1, 1), (3, 1), (2, 0), (2, 1), (0, 1))
+OFFSET = DAMPING / 2
+SHIFT = 1.0 / 64
+
+
+def encode(values):
+    root = values * SHIFT
+    square = root * root
+    fourth = square * square
+    return (fourth * fourth).astype(jnp.bfloat16)
+
+
+def decode(coded):
+    inverse = lax.rsqrt(coded.astype(jnp.float32))
+    square = lax.rsqrt(inverse)
+    return square * lax.rsqrt(square) * (1.0 / SHIFT)
 
 
 def kernel(
     xt_ref, g_ref, w_ref, out_ref,
-    rows, cols, fisher, chain, total, parts, wparts, sums, far, merged,
-    row_s, row_r, col_s, col_r, chain_s, chain_r,
+    rows, cols, fisher, coded, chain, total, parts, wparts, sums, far, merged,
+    row_s, row_r, col_s, col_r, coded_s, coded_r, chain_s, chain_r,
     w_s, w_r, part_s, part_r, far_s, far_r, out_s, out_r,
 ):
     mp = lax.axis_index("mp")
@@ -68,15 +83,48 @@
             device_id_type=MESH,
         )
 
-    def col_copy(k, dy, dc, owner):
+    def row_pass(dy, owner):
+        there = (y + dy) % 4
+        slot = there * 2 + (1 - c if owner else c)
+        return pltpu.make_async_remote_copy(
+            src_ref=rows.at[slot],
+            dst_ref=rows.at[slot],
+            send_sem=row_s.at[there * 2 + 1 - c],
+            recv_sem=row_r.at[slot],
+            device_id=at_y(0, 1)[2],
+            device_id_type=MESH,
+        )
+
+    def col_copy(k, dy, dc):
         there, core, device = at_y(dy, dc)
-        slot = there * 2 + core if owner else me
         return pltpu.make_async_remote_copy(
             src_ref=g_ref.at[:, pl.ds(pl.multiple_of((2 * k + core) * width, width), width)],
+            dst_ref=cols.at[me, k],
+            send_sem=col_s.at[k, there * 2 + core],
+            recv_sem=col_r.at[k, me],
+            device_id=device,
+            device_id_type=MESH,
+        )
+
+    def col_wait(k, slot):
+        pltpu.make_async_remote_copy(
+            src_ref=cols.at[slot, k],
             dst_ref=cols.at[slot, k],
-            send_sem=col_s.at[k, there * 2 + core],
+            send_sem=col_s.at[k, slot],
             recv_sem=col_r.at[k, slot],
-            device_id=device,
+            device_id=at_y(0, 1)[2],
+            device_id_type=MESH,
+        ).wait_recv()
+
+    def col_pass(k, core):
+        step = 1 - 2 * core
+        slot = ((y + 4 - step) % 4) * 2 + core
+        return pltpu.make_async_remote_copy(
+            src_ref=cols.at[slot, k],
+            dst_ref=cols.at[slot, k],
+            send_sem=col_s.at[k, ((y + 2) % 4) * 2 + core],
+            recv_sem=col_r.at[k, slot],
+            device_id=at_y(step + 4, 0)[2],
             device_id_type=MESH,
         )
 
@@ -92,14 +140,20 @@
             device_id_type=MESH,
         )
 
-    for dy, dc in Y_PEERS:
+    def send(i):
+        for dy, dc in ((1, 0), (3, 0), (1, 1), (3, 1), (0, 1)):
+            col_copy(k_of(i), dy, dc).start()
+
+    def forward(i):
+        for core in (0, 1):
+            slot = ((y + 3 + 2 * core) % 4) * 2 + core
+            col_wait(k_of(i), slot)
+            col_pass(k_of(i), core).start()
+
+    for dy, dc in ((1, 0), (3, 0), (2, 0), (0, 1)):
         row_copy(dy, dc, False).start()
-
-    @pl.loop(0, 4)
-    def _(i):
-        for dy, dc in Y_PEERS:
-            col_copy(k_of(i), dy, dc, False).start()
-
+    send(0)
+    send(1)
     for dx in (1, 2, 3):
         w_copy(dx, False).start()
 
@@ -107,16 +161,21 @@
     for k in range(4):
         cols[me, k] = g_ref[:, pl.ds(pl.multiple_of((2 * k + c) * width, width), width)]
     wparts[x] = w_ref[:, x]
-
     fisher[...] = jnp.zeros_like(fisher)
 
-    for dy, dc in Y_PEERS:
-        row_copy(dy, dc, True).wait_recv()
+    for dy in (1, 3, 2):
+        row_copy(dy, 0, True).wait_recv()
+        row_pass(dy, False).start()
+    forward(0)
+    send(2)
+    row_copy(0, 1, True).wait_recv()
+    for dy in (1, 3, 2):
+        row_pass(dy, True).wait_recv()
 
     def compute(i):
         k = k_of(i)
-        for dy, dc in Y_PEERS:
-            col_copy(k, dy, dc, True).wait_recv()
+        for slot in (((y + 3) % 4) * 2 + 1, ((y + 1) % 4) * 2, y * 2 + 1 - c, ((y + 2) % 4) * 2, ((y + 2) % 4) * 2 + 1):
+            col_wait(k, slot)
 
         @pl.loop(0, 8)
         def _(slot):
@@ -126,10 +185,28 @@
                 gradient = jnp.dot(left, right, preferred_element_type=jnp.float32)
                 fisher[4 * h + k] += gradient * gradient
 
-    def chain_copy(way, d, s, source):
+    scale = 1.0 / (seq * 64)
+    main = jnp.where(low, 0, 1)
+    place = jnp.where(low, z, 7 - z)
+
+    def flip(d):
+        return jnp.where(low, d, 7 - d)
+
+    def coded_copy(way, d, s):
         span = pl.ds(s * piece, piece)
         return pltpu.make_async_remote_copy(
-            src_ref=source.at[span],
+            src_ref=coded.at[way, d, span],
+            dst_ref=coded.at[way, d, span],
+            send_sem=coded_s.at[way, d, s],
+            recv_sem=coded_r.at[way, d, s],
+            device_id=at_z(1 - 2 * way),
+            device_id_type=MESH,
+        )
+
+    def chain_copy(way, d, s):
+        span = pl.ds(s * piece, piece)
+        return pltpu.make_async_remote_copy(
+            src_ref=chain.at[way, d, span],
             dst_ref=chain.at[way, d, span],
             send_sem=chain_s.at[way, d, s],
             recv_sem=chain_r.at[way, d, s],
@@ -137,48 +214,85 @@
             device_id_type=MESH,
         )
 
-    def chain_step(way, d):
-        ahead = (d - z) * (1 - 2 * way)
-        first = z == 7 * way
-
-        @pl.when(jnp.logical_and(first, ahead > 0))
-        def _():
-            for s in range(SUBS):
-                chain_copy(way, d, s, fisher.at[d]).start()
-
-        @pl.when(jnp.logical_and(jnp.logical_not(first), ahead > 0))
+    def main_step(away):
+        d = flip(away)
+
+        @pl.when(place == 0)
         def _():
             for s in range(SUBS):
                 span = slice(s * piece, (s + 1) * piece)
-                chain_copy(way, d, s, chain.at[way, d]).wait_recv()
-                chain[way, d, span] += fisher[d, span]
-                chain_copy(way, d, s, chain.at[way, d]).start()
-
-    main = jnp.where(low, 0, 1)
-    place = jnp.where(low, z, 7 - z)
-
-    def flip(d):
-        return jnp.where(low, d, 7 - d)
-
-    for i in range(4):
-        compute(i)
-
+                coded[main, d, span] = encode(fisher[d, span] * scale + OFFSET)
+                coded_copy(main, d, s).start()
+
+        @pl.when(jnp.logical_and(place > 0, place < away))
+        def _():
+            for s in range(SUBS):
+                span = slice(s * piece, (s + 1) * piece)
+                coded_copy(main, d, s).wait_recv()
+                coded[main, d, span] = encode(decode(coded[main, d, span]) + fisher[d, span] * scale)
+                coded_copy(main, d, s).start()
+
+    def back_step(away):
+        d = flip(away)
+
+        @pl.when(place == 3)
+        def _():
+            for s in range(SUBS):
+                span = slice(s * piece, (s + 1) * piece)
+                coded_copy(1 - main, d, s).wait_recv()
+                chain[1 - main, d, span] = decode(coded[1 - main, d, span]) + fisher[d, span] * scale
+                chain_copy(1 - main, d, s).start()
+
+        @pl.when(jnp.logical_and(place < 3, place > away))
+        def _():
+            for s in range(SUBS):
+                span = slice(s * piece, (s + 1) * piece)
+                chain_copy(1 - main, d, s).wait_recv()
+                chain[1 - main, d, span] += fisher[d, span] * scale
+                chain_copy(1 - main, d, s).start()
+
+    def end_steps(*away):
         @pl.when(place == 0)
         def _():
-            chain_step(main, flip(7 - i))
-
-        if i > 0:
-            @pl.when(place > 0)
-            def _():
-                chain_step(main, flip(8 - i))
-
-    @pl.when(place > 0)
+            for one in away:
+                main_step(one)
+
+    def inner_steps(*away):
+        @pl.when(place > 0)
+        def _():
+            for one in away:
+                main_step(one)
+
+    forward(1)
+    send(3)
+    compute(0)
+    end_steps(7, 3)
+    forward(2)
+    compute(1)
+    end_steps(6)
+    inner_steps(7)
+    forward(3)
+    compute(2)
+    end_steps(5)
+    inner_steps(3)
+    compute(3)
+    end_steps(4, 2, 1)
+    inner_steps(6)
+
+    @pl.when(place > 1)
     def _():
-        chain_step(main, flip(4))
-
-    for i in range(3):
-        chain_step(1 - main, flip(i))
-        chain_step(main, flip(3 - i))
+        back_step(0)
+
+    inner_steps(5)
+
+    @pl.when(place == 1)
+    def _():
+        back_step(0)
+
+    back_step(1)
+    inner_steps(4)
+    back_step(2)
+    inner_steps(2)
 
     def part_copy(s, dx, owner):
         there, device = at_x(dx)
@@ -214,17 +328,34 @@
             device_id_type=MESH,
         )
 
-    scale = 1.0 / (seq * 64)
     for s in range(SUBS):
-        span = slice(s * piece, (s + 1) * piece)
-        for q in range(4):
-            total[s, q] = fisher[z, s * piece + q * band:s * piece + (q + 1) * band]
-        for way in (0, 1):
-            @pl.when(z != 7 * way)
-            def _():
-                chain_copy(way, z, s, chain.at[way, z]).wait_recv()
-                for q in range(4):
-                    total[s, q] += chain[way, z, s * piece + q * band:s * piece + (q + 1) * band]
+        base = s * piece
+
+        @pl.when(place == 0)
+        def _():
+            chain_copy(1 - main, z, s).wait_recv()
+            for q in range(4):
+                span = slice(base + q * band, base + (q + 1) * band)
+                total[s, q] = fisher[z, span] * scale + OFFSET + chain[1 - main, z, span]
+
+        @pl.when(jnp.logical_and(place > 0, place < 3))
+        def _():
+            coded_copy(main, z, s).wait_recv()
+            chain_copy(1 - main, z, s).wait_recv()
+            for q in range(4):
+                span = slice(base + q * band, base + (q + 1) * band)
+                total[s, q] = fisher[z, span] * scale + decode(coded[main, z, span]) + chain[1 - main, z, span]
+
+        @pl.when(place == 3)
+        def _():
+            coded_copy(main, z, s).wait_recv()
+            coded_copy(1 - main, z, s).wait_recv()
+            for q in range(4):
+                span = slice(base + q * band, base + (q + 1) * band)
+                total[s, q] = (
+                    fisher[z, span] * scale + decode(coded[main, z, span]) + decode(coded[1 - main, z, span])
+                )
+
         for dx in (1, 2, 3):
             part_copy(s, dx, False).start()
         parts[s, x] = total[s, x]
@@ -234,7 +365,7 @@
     for s in range(SUBS):
         for dx in (1, 2, 3):
             part_copy(s, dx, True).wait_recv()
-        damped = [parts[s, m] * scale + DAMPING for m in range(4)]
+        damped = [parts[s, m] for m in range(4)]
         product = [damped[m] * wparts[m, s] for m in range(4)]
         sums[s, 0] = (product[0] + product[1]) + (product[2] + product[3])
         sums[s, 1] = (damped[0] + damped[1]) + (damped[2] + damped[3])
@@ -249,13 +380,17 @@
             out_copy(s, dx, True).wait_recv()
     out_ref[...] = merged[...]
 
-    for dy, dc in Y_PEERS:
+    for dy, dc in ((1, 0), (3, 0), (2, 0), (0, 1)):
         row_copy(dy, dc, False).wait_send()
+    for dy in (1, 3, 2):
+        row_pass(dy, False).wait_send()
 
     @pl.loop(0, 4)
     def _(k):
-        for dy, dc in Y_PEERS:
-            col_copy(k, dy, dc, False).wait_send()
+        for dy, dc in ((1, 0), (3, 0), (1, 1), (3, 1), (0, 1)):
+            col_copy(k, dy, dc).wait_send()
+        for core in (0, 1):
+            col_pass(k, core).wait_send()
 
     for dx in (1, 2, 3):
         w_copy(dx, False).wait_send()
@@ -266,12 +401,16 @@
         far_copy(s).wait_send()
 
     @pl.loop(0, 8)
-    def _(d):
-        for way in (0, 1):
-            @pl.when((d - z) * (1 - 2 * way) > 0)
-            def _():
-                for s in range(SUBS):
-                    chain_copy(way, d, s, fisher.at[d]).wait_send()
+    def _(away):
+        @pl.when(away > place)
+        def _():
+            for s in range(SUBS):
+                coded_copy(main, flip(away), s).wait_send()
+
+        @pl.when(away < place)
+        def _():
+            for s in range(SUBS):
+                chain_copy(1 - main, flip(away), s).wait_send()
 
 
 def shards(inputs, cotangent, token_ids, weights):
@@ -293,6 +432,7 @@
             pltpu.VMEM((8, 2 * height, seq), jnp.bfloat16),
             pltpu.VMEM((8, 4, seq, width), jnp.bfloat16),
             pltpu.VMEM((8, height, width), jnp.float32),
+            pltpu.VMEM((2, 8, height, width), jnp.bfloat16),
             pltpu.VMEM((2, 8, height, width), jnp.float32),
             pltpu.VMEM((SUBS, 4, band, width), jnp.float32),
             pltpu.VMEM((SUBS, 4, band, width), jnp.float32),
@@ -301,7 +441,7 @@
             pltpu.VMEM((SUBS, 2, band, width), jnp.float32),
             pltpu.VMEM((SUBS, 4, band, width), jnp.float32),
             dma((8,)), dma((8,)), dma((4, 8)), dma((4, 8)),
-            dma((2, 8, SUBS)), dma((2, 8, SUBS)),
+            dma((2, 8, SUBS)), dma((2, 8, SUBS)), dma((2, 8, SUBS)), dma((2, 8, SUBS)),
             dma((4,)), dma((4,)), dma((SUBS, 4)), dma((SUBS, 4)),
             dma((SUBS,)), dma((SUBS,)), dma((SUBS, 4)), dma((SUBS, 4)),
         ],

time: 185 us -> 155 us (0.84)
  the two profiles are of different devices: /device:TPU:64 before, /device:TPU:88 now
where the time goes in v2:
time: 155 us; the launch traced here: 154 us
  Pallas kernels  150 us (97%)
  local copies, waits for them, and re-layouts  3.83 us (2%)
    pallas_call x1, Pallas kernels, shards(): pl.pallas_call(kernel, out_shape=jax.ShapeDtypeStruct((SUBS, 4, band, wid...  150 us
    unnamed x8, local copies, waits for them, and re-layouts  3.83 us

profile of v2, /device:TPU:88, one launch (start us, length us, event | category | flops | bytes accessed | tf_op | source)
XLA Modules:
  0.0 154.3 jit_solution(6428129501155028100)
XLA Ops:
  0.0 0.0 copy-start.2
  0.0 0.7 copy-done.2
  0.7 0.0 copy-start
  0.7 1.4 copy.5
  2.1 0.0 copy-start.1
  2.1 0.0 copy-done
  2.1 1.0 copy-done.1
  3.1 150.4 %shard_map.46 = f32[4,4,16,512]{3,2,1,0:T(8,128)S(1)} custom-call(bf16[2048,128]{1,0:T(8,128)(2,1)S(1)} %fusion.xt_ref, bf16[128,4096]{1,0:T(8,128)(2,1)S(1)} %bitcast.12, f32[4,4,16,512]{3,2,1,0:T(8,128)S(1)} %bitcast.13), custom_call_target="tpu_custom_call" | custom-call | tf_op jit(solution)/shard_map/pallas_call | solution.py:426
  153.5 0.8 copy.7
  (2 shorter events, 0.0 us)
Async XLA Ops:
  0.0 0.7 copy-start.2
  0.7 1.5 copy-start
  2.1 1.0 copy-start.1

commit v3 on v2

--- a/solution.py
+++ b/solution.py
@@ -11,28 +11,40 @@
 MESH = pl.DeviceIdType.MESH
 Y_PEERS = ((1, 0), (3, 0), (1, 1), (3, 1), (2, 0), (2, 1), (0, 1))
 OFFSET = DAMPING / 2
-SHIFT = 1.0 / 64
+MIDDLE = 90.5
+LOW_UNIT = 2.0
+HIGH_UNIT = 4096.0
 
 
 def encode(values):
-    root = values * SHIFT
-    square = root * root
+    small = values < MIDDLE
+    ratio = values * jnp.where(small, 1.0 / LOW_UNIT, 1.0 / HIGH_UNIT)
+    square = ratio * ratio
     fourth = square * square
-    return (fourth * fourth).astype(jnp.bfloat16)
-
-
-def decode(coded):
-    inverse = lax.rsqrt(coded.astype(jnp.float32))
-    square = lax.rsqrt(inverse)
-    return square * lax.rsqrt(square) * (1.0 / SHIFT)
+    eighth = fourth * fourth
+    power = (eighth * eighth) * (fourth * square)
+    return jnp.where(small, power, -power).astype(jnp.bfloat16)
+
+
+def decode(code):
+    power = code.astype(jnp.float32)
+    ratio = jnp.exp2(jnp.log2(jnp.abs(power)) * (1.0 / 22))
+    return ratio * jnp.where(power > 0, LOW_UNIT, HIGH_UNIT)
 
 
 def kernel(
-    xt_ref, g_ref, w_ref, out_ref,
-    rows, cols, fisher, coded, chain, total, parts, wparts, sums, far, merged,
-    row_s, row_r, col_s, col_r, coded_s, coded_r, chain_s, chain_r,
+    xt_ref, g_hbm, w_hbm, out_ref,
+    g_ref, w_ref, rows, cols, fisher, coded, total, parts, wparts,
+    tops, bottoms, far_tops, far_bottoms, merged, load_s,
+    row_s, row_r, col_s, col_r, coded_s, coded_r,
     w_s, w_r, part_s, part_r, far_s, far_r, out_s, out_r,
 ):
+    loads = (
+        pltpu.make_async_copy(g_hbm, g_ref, load_s.at[0]),
+        pltpu.make_async_copy(w_hbm, w_ref, load_s.at[1]),
+    )
+    for load in loads:
+        load.start()
     mp = lax.axis_index("mp")
     tok = lax.axis_index("tok")
     x, zh = mp // 2, mp % 2
@@ -66,6 +78,9 @@
         pl.semaphore_signal(barrier, 1, device_id=at_z(dz), device_id_type=MESH)
     pl.semaphore_wait(barrier, len(Y_PEERS) + 6)
 
+    for load in loads:
+        load.wait()
+
     low = z < 4
 
     def k_of(i):
@@ -141,8 +156,10 @@
         )
 
     def send(i):
-        for dy, dc in ((1, 0), (3, 0), (1, 1), (3, 1), (0, 1)):
-            col_copy(k_of(i), dy, dc).start()
+        for back in (0, 1):
+            for dc in (0, 1):
+                col_copy(k_of(i), 1 + 2 * ((c + back) % 2), dc).start()
+        col_copy(k_of(i), 0, 1).start()
 
     def forward(i):
         for core in (0, 1):
@@ -153,7 +170,6 @@
     for dy, dc in ((1, 0), (3, 0), (2, 0), (0, 1)):
         row_copy(dy, dc, False).start()
     send(0)
-    send(1)
     for dx in (1, 2, 3):
         w_copy(dx, False).start()
 
@@ -167,7 +183,7 @@
         row_copy(dy, 0, True).wait_recv()
         row_pass(dy, False).start()
     forward(0)
-    send(2)
+    send(1)
     row_copy(0, 1, True).wait_recv()
     for dy in (1, 3, 2):
         row_pass(dy, True).wait_recv()
@@ -203,96 +219,59 @@
             device_id_type=MESH,
         )
 
-    def chain_copy(way, d, s):
-        span = pl.ds(s * piece, piece)
-        return pltpu.make_async_remote_copy(
-            src_ref=chain.at[way, d, span],
-            dst_ref=chain.at[way, d, span],
-            send_sem=chain_s.at[way, d, s],
-            recv_sem=chain_r.at[way, d, s],
-            device_id=at_z(1 - 2 * way),
-            device_id_type=MESH,
-        )
-
-    def main_step(away):
+    def piece_of(s):
+        return pl.ds(pl.multiple_of(s * piece, piece), piece)
+
+    def first_step(away):
         d = flip(away)
 
-        @pl.when(place == 0)
+        @pl.loop(0, SUBS)
+        def _(s):
+            coded[main, d, piece_of(s)] = encode(fisher[d, piece_of(s)] * scale + OFFSET)
+            coded_copy(main, d, s).start()
+
+    def step(way, away):
+        d = flip(away)
+
+        @pl.loop(0, SUBS)
+        def _(s):
+            coded_copy(way, d, s).wait_recv()
+            own = fisher[d, piece_of(s)] * scale
+            coded[way, d, piece_of(s)] = encode(decode(coded[way, d, piece_of(s)]) + own)
+            coded_copy(way, d, s).start()
+
+    def steps(where, *aways):
+        @pl.when(place == where)
         def _():
-            for s in range(SUBS):
-                span = slice(s * piece, (s + 1) * piece)
-                coded[main, d, span] = encode(fisher[d, span] * scale + OFFSET)
-                coded_copy(main, d, s).start()
-
-        @pl.when(jnp.logical_and(place > 0, place < away))
-        def _():
-            for s in range(SUBS):
-                span = slice(s * piece, (s + 1) * piece)
-                coded_copy(main, d, s).wait_recv()
-                coded[main, d, span] = encode(decode(coded[main, d, span]) + fisher[d, span] * scale)
-                coded_copy(main, d, s).start()
-
-    def back_step(away):
-        d = flip(away)
-
-        @pl.when(place == 3)
-        def _():
-            for s in range(SUBS):
-                span = slice(s * piece, (s + 1) * piece)
-                coded_copy(1 - main, d, s).wait_recv()
-                chain[1 - main, d, span] = decode(coded[1 - main, d, span]) + fisher[d, span] * scale
-                chain_copy(1 - main, d, s).start()
-
-        @pl.when(jnp.logical_and(place < 3, place > away))
-        def _():
-            for s in range(SUBS):
-                span = slice(s * piece, (s + 1) * piece)
-                chain_copy(1 - main, d, s).wait_recv()
-                chain[1 - main, d, span] += fisher[d, span] * scale
-                chain_copy(1 - main, d, s).start()
-
-    def end_steps(*away):
-        @pl.when(place == 0)
-        def _():
-            for one in away:
-                main_step(one)
-
-    def inner_steps(*away):
-        @pl.when(place > 0)
-        def _():
-            for one in away:
-                main_step(one)
-
+            for away in aways:
+                if where == 0:
+                    first_step(away)
+                elif away < 0:
+                    step(1 - main, -away % 8)
+                else:
+                    step(main, away)
+
+    compute(0)
+    steps(0, 7, 3)
     forward(1)
+    send(2)
+    compute(1)
+    steps(0, 6)
+    forward(2)
     send(3)
-    compute(0)
-    end_steps(7, 3)
-    forward(2)
-    compute(1)
-    end_steps(6)
-    inner_steps(7)
+    steps(1, 7, 3)
+    steps(2, 7)
+    compute(2)
+    steps(0, 5)
     forward(3)
-    compute(2)
-    end_steps(5)
-    inner_steps(3)
+    steps(1, 6)
+    steps(2, 3)
+    steps(3, 7)
     compute(3)
-    end_steps(4, 2, 1)
-    inner_steps(6)
-
-    @pl.when(place > 1)
-    def _():
-        back_step(0)
-
-    inner_steps(5)
-
-    @pl.when(place == 1)
-    def _():
-        back_step(0)
-
-    back_step(1)
-    inner_steps(4)
-    back_step(2)
-    inner_steps(2)
+    steps(0, 4, 2, 1)
+    steps(1, 5, -8, 4, 2)
+    steps(2, 6, -8, 5, -1, 4)
+    steps(3, -8, 6, -1, 5, -2, 4)
 
     def part_copy(s, dx, owner):
         there, device = at_x(dx)
@@ -306,15 +285,18 @@
             device_id_type=MESH,
         )
 
-    def far_copy(s):
-        return pltpu.make_async_remote_copy(
-            src_ref=sums.at[s],
-            dst_ref=far.at[s],
-            send_sem=far_s.at[s],
-            recv_sem=far_r.at[s],
-            device_id=at_z(8),
-            device_id_type=MESH,
-        )
+    def far_copies(s):
+        return [
+            pltpu.make_async_remote_copy(
+                src_ref=here.at[s],
+                dst_ref=there.at[s],
+                send_sem=far_s.at[kind, s],
+                recv_sem=far_r.at[kind, s],
+                device_id=at_z(8),
+                device_id_type=MESH,
+            )
+            for kind, (here, there) in enumerate(((tops, far_tops), (bottoms, far_bottoms)))
+        ]
 
     def out_copy(s, dx, owner):
         there, device = at_x(dx)
@@ -330,26 +312,17 @@
 
     for s in range(SUBS):
         base = s * piece
+        coded_copy(1 - main, z, s).wait_recv()
 
         @pl.when(place == 0)
         def _():
-            chain_copy(1 - main, z, s).wait_recv()
             for q in range(4):
                 span = slice(base + q * band, base + (q + 1) * band)
-                total[s, q] = fisher[z, span] * scale + OFFSET + chain[1 - main, z, span]
-
-        @pl.when(jnp.logical_and(place > 0, place < 3))
+                total[s, q] = fisher[z, span] * scale + OFFSET + decode(coded[1 - main, z, span])
+
+        @pl.when(place > 0)
         def _():
             coded_copy(main, z, s).wait_recv()
-            chain_copy(1 - main, z, s).wait_recv()
-            for q in range(4):
-                span = slice(base + q * band, base + (q + 1) * band)
-                total[s, q] = fisher[z, span] * scale + decode(coded[main, z, span]) + chain[1 - main, z, span]
-
-        @pl.when(place == 3)
-        def _():
-            coded_copy(main, z, s).wait_recv()
-            coded_copy(1 - main, z, s).wait_recv()
             for q in range(4):
                 span = slice(base + q * band, base + (q + 1) * band)
                 total[s, q] = (
@@ -367,12 +340,15 @@
             part_copy(s, dx, True).wait_recv()
         damped = [parts[s, m] for m in range(4)]
         product = [damped[m] * wparts[m, s] for m in range(4)]
-        sums[s, 0] = (product[0] + product[1]) + (product[2] + product[3])
-        sums[s, 1] = (damped[0] + damped[1]) + (damped[2] + damped[3])
-        far_copy(s).start()
+        tops[s] = (product[0] + product[1]) + (product[2] + product[3])
+        bottoms[s] = encode(((damped[0] + damped[1]) + (damped[2] + damped[3])) * 0.25)
+        for copy in far_copies(s):
+            copy.start()
     for s in range(SUBS):
-        far_copy(s).wait_recv()
-        merged[s, x] = (sums[s, 0] + far[s, 0]) / (sums[s, 1] + far[s, 1])
+        for copy in far_copies(s):
+            copy.wait_recv()
+        bottom = decode(bottoms[s]) + decode(far_bottoms[s])
+        merged[s, x] = (tops[s] + far_tops[s]) * 0.25 / bottom
         for dx in (1, 2, 3):
             out_copy(s, dx, False).start()
     for s in range(SUBS):
@@ -398,19 +374,15 @@
             part_copy(s, dx, False).wait_send()
             out_copy(s, dx, False).wait_send()
     for s in range(SUBS):
-        far_copy(s).wait_send()
+        for copy in far_copies(s):
+            copy.wait_send()
 
     @pl.loop(0, 8)
     def _(away):
-        @pl.when(away > place)
+        @pl.when(away != place)
         def _():
             for s in range(SUBS):
-                coded_copy(main, flip(away), s).wait_send()
-
-        @pl.when(away < place)
-        def _():
-            for s in range(SUBS):
-                chain_copy(1 - main, flip(away), s).wait_send()
+                coded_copy(jnp.where(away > place, main, 1 - main), flip(away), s).wait_send()
 
 
 def shards(inputs, cotangent, token_ids, weights):
@@ -426,24 +398,28 @@
     merged = pl.pallas_call(
         kernel,
         out_shape=jax.ShapeDtypeStruct((SUBS, 4, band, width), jnp.float32),
-        in_specs=[vmem] * 3,
+        in_specs=[vmem, pl.BlockSpec(memory_space=pl.ANY), pl.BlockSpec(memory_space=pl.ANY)],
         out_specs=vmem,
         scratch_shapes=[
+            pltpu.VMEM((seq, query), jnp.bfloat16),
+            pltpu.VMEM((SUBS, 4, band, width), jnp.float32),
             pltpu.VMEM((8, 2 * height, seq), jnp.bfloat16),
             pltpu.VMEM((8, 4, seq, width), jnp.bfloat16),
             pltpu.VMEM((8, height, width), jnp.float32),
             pltpu.VMEM((2, 8, height, width), jnp.bfloat16),
-            pltpu.VMEM((2, 8, height, width), jnp.float32),
             pltpu.VMEM((SUBS, 4, band, width), jnp.float32),
             pltpu.VMEM((SUBS, 4, band, width), jnp.float32),
             pltpu.VMEM((4, SUBS, band, width), jnp.float32),
-            pltpu.VMEM((SUBS, 2, band, width), jnp.float32),
-            pltpu.VMEM((SUBS, 2, band, width), jnp.float32),
+            pltpu.VMEM((SUBS, band, width), jnp.float32),
+            pltpu.VMEM((SUBS, band, width), jnp.bfloat16),
+            pltpu.VMEM((SUBS, band, width), jnp.float32),
+            pltpu.VMEM((SUBS, band, width), jnp.bfloat16),
             pltpu.VMEM((SUBS, 4, band, width), jnp.float32),
+            dma((2,)),
             dma((8,)), dma((8,)), dma((4, 8)), dma((4, 8)),
-            dma((2, 8, SUBS)), dma((2, 8, SUBS)), dma((2, 8, SUBS)), dma((2, 8, SUBS)),
+            dma((2, 8, SUBS)), dma((2, 8, SUBS)),
             dma((4,)), dma((4,)), dma((SUBS, 4)), dma((SUBS, 4)),
-            dma((SUBS,)), dma((SUBS,)), dma((SUBS, 4)), dma((SUBS, 4)),
+            dma((2, SUBS)), dma((2, SUBS)), dma((SUBS, 4)), dma((SUBS, 4)),
         ],
         compiler_params=pltpu.CompilerParams(
             collective_id=0, has_side_effects=True, vmem_limit_bytes=48 * 1024 * 1024

time: 155 us -> 123 us (0.79)
  the two profiles are of different devices: /device:TPU:88 before, /device:TPU:120 now
where the time goes in v3:
time: 123 us; the launch traced here: 122 us
  Pallas kernels  119 us (97%)
  local copies, waits for them, and re-layouts  3.83 us (3%)
    pallas_call x1, Pallas kernels, shards(): pl.pallas_call(kernel, out_shape=jax.ShapeDtypeStruct((SUBS, 4, band, wid...  119 us
    unnamed x8, local copies, waits for them, and re-layouts  3.83 us

profile of v3, /device:TPU:120, one launch (start us, length us, event | category | flops | bytes accessed | tf_op | source)
XLA Modules:
  0.0 122.5 jit_solution(18407374661071228506)
XLA Ops:
  0.0 0.0 copy-start.2
  0.0 0.7 copy-done.2
  0.7 0.0 copy-start
  0.7 1.4 %copy.5 = bf16[1,1,128,2048]{2,3,1,0:T(8,128)(2,1)S(1)} copy(bf16[1,1,128,2048]{3,2,1,0:T(8,128)(2,1)} %param.4) | data formatting | bytes 1048576 | tf_op args[0]
  2.1 0.0 copy-start.1
  2.1 0.0 copy-done
  2.1 1.0 copy-done.1
  3.1 118.6 %shard_map.46 = f32[4,4,16,512]{3,2,1,0:T(8,128)S(1)} custom-call(bf16[2048,128]{1,0:T(8,128)(2,1)S(1)} %fusion.xt_ref, bf16[128,4096]{1,0:T(8,128)(2,1)S(1)} %bitcast.12, f32[4,4,16,512]{3,2,1,0:T(8,128)S(1)} %bitcast.13), custom_call_target="tpu_custom_call" | custom-call | tf_op jit(solution)/shard_map/pallas_call | solution.py:398
  121.7 0.8 copy.7
  (2 shorter events, 0.0 us)
Async XLA Ops:
  0.0 0.7 copy-start.2
  0.7 1.5 %copy-start = (bf16[1,1,128,4096]{3,2,1,0:T(8,128)(2,1)S(1)}, bf16[1,1,128,4096]{3,2,1,0:T(8,128)(2,1)}, u32[]{:S(2)}) copy-start(bf16[1,1,128,4096]{3,2,1,0:T(8,128)(2,1)} %param.5) | copy-start | bytes 3145732
  2.1 1.0 copy-start.1

commit v4 on v3

v4 whole, which is shorter than its diff:
```python
import jax
import jax.numpy as jnp
from jax import lax
from jax.experimental import pallas as pl
from jax.experimental.pallas import tpu as pltpu
from jax.sharding import PartitionSpec as P

FIRST_TEXT = 37984
DAMPING = 0.1
ROUNDS = 2
SUBS = 2
MESH = pl.DeviceIdType.MESH
Y_PEERS = ((1, 0), (3, 0), (1, 1), (3, 1), (2, 0), (2, 1), (0, 1))
OFFSET = DAMPING / 2
MIDDLE = 90.5
LOW_UNIT = 2.0
HIGH_UNIT = 4096.0


def encode(values):
    small = values < MIDDLE
    ratio = values * jnp.where(small, 1.0 / LOW_UNIT, 1.0 / HIGH_UNIT)
    square = ratio * ratio
    fourth = square * square
    eighth = fourth * fourth
    power = (eighth * eighth) * (fourth * square)
    return jnp.where(small, power, -power).astype(jnp.bfloat16)


def decode(code):
    power = code.astype(jnp.float32)
    ratio = jnp.exp2(jnp.log2(jnp.abs(power)) * (1.0 / 22))
    return ratio * jnp.where(power > 0, LOW_UNIT, HIGH_UNIT)


def kernel(
    x_hbm, g_hbm, w_hbm, ids_ref, out_ref,
    x_ref, xt_ref, g_ref, w_ref, rows, cols, fisher, coded, total, parts, wparts,
    tops, bottoms, far_tops, far_bottoms, merged, load_s,
    row_s, row_r, col_s, col_r, coded_s, coded_r,
    w_s, w_r, part_s, part_r, far_s, far_r, out_s, out_r,
):
    loads = (
        pltpu.make_async_copy(x_hbm, x_ref, load_s.at[0]),
        pltpu.make_async_copy(g_hbm, g_ref, load_s.at[1]),
        pltpu.make_async_copy(w_hbm, w_ref, load_s.at[2]),
    )
    for load in loads:
        load.start()
    mp = lax.axis_index("mp")
    tok = lax.axis_index("tok")
    x, zh = mp // 2, mp % 2
    y, z, c = tok // 16, (tok // 2) % 8, tok % 2
    me = y * 2 + c
    seq = g_ref.shape[0]
    width = w_ref.shape[3]
    height, part = fisher.shape[1:]
    piece = height // SUBS
    band = piece // 4

    def at_y(dy, dc):
        there = (y + dy) % 4
        core = 1 - c if dc else c
        return there, core, (mp, (there * 8 + z) * 2 + core)

    def at_x(dx):
        there = (x + dx) % 4
        return there, (there * 2 + zh, tok)

    def at_z(dz):
        deep = zh * 8 + z + dz + 16
        return (x * 2 + (deep // 8) % 2, (y * 8 + deep % 8) * 2 + c)

    barrier = pltpu.get_barrier_semaphore()
    for dy, dc in Y_PEERS:
        pl.semaphore_signal(barrier, 1, device_id=at_y(dy, dc)[2], device_id_type=MESH)
    for dx in (1, 2, 3):
        pl.semaphore_signal(barrier, 1, device_id=at_x(dx)[1], device_id_type=MESH)
    for dz in (1, -1, 8):
        pl.semaphore_signal(barrier, 1, device_id=at_z(dz), device_id_type=MESH)
    loads[0].wait()
    kept = ids_ref[...] >= FIRST_TEXT
    for r in range(8):
        some = x_ref[:, r * height:(r + 1) * height].astype(jnp.float32).T
        xt_ref[r * height:(r + 1) * height, :] = jnp.where(kept, some, 0.0).astype(jnp.bfloat16)

    pl.semaphore_wait(barrier, len(Y_PEERS) + 6)

    for load in loads[1:]:
        load.wait()

    low = z < 4

    def unit_of(u):
        return u // 4 * 4 + jnp.where(low, 3 - u % 4, u % 4)

    def row_copy(dy, dc, owner):
        there, core, device = at_y(dy, dc)
        slot = there * 2 + core if owner else me
        return pltpu.make_async_remote_copy(
            src_ref=xt_ref.at[pl.ds(there * 2 * height, 2 * height)],
            dst_ref=rows.at[slot],
            send_sem=row_s.at[there * 2 + core],
            recv_sem=row_r.at[slot],
            device_id=device,
            device_id_type=MESH,
        )

    def row_pass(dy, owner):
        there = (y + dy) % 4
        slot = there * 2 + (1 - c if owner else c)
        return pltpu.make_async_remote_copy(
            src_ref=rows.at[slot],
            dst_ref=rows.at[slot],
            send_sem=row_s.at[there * 2 + 1 - c],
            recv_sem=row_r.at[slot],
            device_id=at_y(0, 1)[2],
            device_id_type=MESH,
        )

    def col_copy(k, dy, dc):
        there, core, device = at_y(dy, dc)
        return pltpu.make_async_remote_copy(
            src_ref=g_ref.at[:, pl.ds(pl.multiple_of((2 * (k % 4) + core) * width + k // 4 * part, part), part)],
            dst_ref=cols.at[me, k],
            send_sem=col_s.at[k, there * 2 + core],
            recv_sem=col_r.at[k, me],
            device_id=device,
            device_id_type=MESH,
        )

    def col_wait(k, slot):
        pltpu.make_async_remote_copy(
            src_ref=cols.at[slot, k],
            dst_ref=cols.at[slot, k],
            send_sem=col_s.at[k, slot],
            recv_sem=col_r.at[k, slot],
            device_id=at_y(0, 1)[2],
            device_id_type=MESH,
        ).wait_recv()

    def col_pass(k, core):
        step = 1 - 2 * core
        slot = ((y + 4 - step) % 4) * 2 + core
        return pltpu.make_async_remote_copy(
            src_ref=cols.at[slot, k],
            dst_ref=cols.at[slot, k],
            send_sem=col_s.at[k, ((y + 2) % 4) * 2 + core],
            recv_sem=col_r.at[k, slot],
            device_id=at_y(step + 4, 0)[2],
            device_id_type=MESH,
        )

    def w_copy(dx, owner):
        there, device = at_x(dx)
        slot = there if owner else x
        return pltpu.make_async_remote_copy(
            src_ref=w_ref.at[:, there],
            dst_ref=wparts.at[slot],
            send_sem=w_s.at[there],
            recv_sem=w_r.at[slot],
            device_id=device,
            device_id_type=MESH,
        )

    def send(u):
        for dy, dc in ((1, 0), (3, 0), (1, 1), (3, 1), (0, 1)):
            col_copy(unit_of(u), dy, dc).start()

    def forward(u):
        for core in (0, 1):
            slot = ((y + 3 + 2 * core) % 4) * 2 + core
            col_wait(unit_of(u), slot)
            col_pass(unit_of(u), core).start()

    for dy, dc in ((1, 0), (3, 0), (2, 0), (0, 1)):
        row_copy(dy, dc, False).start()
    send(0)
    send(1)
    for dx in (1, 2, 3):
        w_copy(dx, False).start()

    rows[me] = xt_ref[pl.ds(y * 2 * height, 2 * height), :]
    for k in range(4 * ROUNDS):
        start = pl.multiple_of((2 * (k % 4) + c) * width + k // 4 * part, part)
        cols[me, k] = g_ref[:, pl.ds(start, part)]
    wparts[x] = w_ref[:, x]

    for dy in (1, 3, 2):
        row_copy(dy, 0, True).wait_recv()
        row_pass(dy, False).start()
    forward(0)
    send(2)
    row_copy(0, 1, True).wait_recv()
    for dy in (1, 3, 2):
        row_pass(dy, True).wait_recv()

    def arrived(u):
        k = unit_of(u)
        for slot in (((y + 3) % 4) * 2 + 1, ((y + 1) % 4) * 2, y * 2 + 1 - c, ((y + 2) % 4) * 2, ((y + 2) % 4) * 2 + 1):
            col_wait(k, slot)

    scale = 1.0 / (seq * 64)
    main = jnp.where(low, 0, 1)
    place = jnp.where(low, z, 7 - z)

    def flip(d):
        return jnp.where(low, d, 7 - d)

    def coded_copy(way, d, s):
        span = pl.ds(s * piece, piece)
        return pltpu.make_async_remote_copy(
            src_ref=coded.at[way, d, span],
            dst_ref=coded.at[way, d, span],
            send_sem=coded_s.at[way, d, s],
            recv_sem=coded_r.at[way, d, s],
            device_id=at_z(1 - 2 * way),
            device_id_type=MESH,
        )

    def piece_of(s):
        return pl.ds(pl.multiple_of(s * piece, piece), piece)

    def first_step(r, away):
        d = r * 8 + flip(away)

        @pl.loop(0, SUBS)
        def _(s):
            coded[main, d, piece_of(s)] = encode(fisher[d, piece_of(s)] * scale + OFFSET)
            coded_copy(main, d, s).start()

    def step(way, r, away):
        d = r * 8 + flip(away)

        @pl.loop(0, SUBS)
        def _(s):
            coded_copy(way, d, s).wait_recv()
            own = fisher[d, piece_of(s)] * scale
            coded[way, d, piece_of(s)] = encode(decode(coded[way, d, piece_of(s)]) + own)
            coded_copy(way, d, s).start()

    def block(u, away, early):
        d = u // 4 * 8 + flip(away)
        k = unit_of(u)
        base = flip(away) // 4 * height

        @pl.loop(0, SUBS)
        def _(s):
            summed = None
            for slot in range(8):
                left = rows[slot, pl.ds(pl.multiple_of(base + s * piece, piece), piece), :]
                gradient = jnp.dot(left, cols[slot, k], preferred_element_type=jnp.float32)
                square = gradient * gradient
                summed = square if summed is None else summed + square
            fisher[d, piece_of(s)] = summed
            if early:
                @pl.when(place == 0)
                def _():
                    coded[main, d, piece_of(s)] = encode(summed * scale + OFFSET)
                    coded_copy(main, d, s).start()

    def steps(where, r, *aways):
        @pl.when(place == where)
        def _():
            for away in aways:
                if where == 0:
                    first_step(r, away)
                elif away < 0:
                    step(1 - main, r, -away % 8)
                else:
                    step(main, r, away)

    forward(1)
    send(3)
    arrived(0)
    block(0, 7, True)
    block(0, 3, True)
    forward(2)
    send(4)
    arrived(1)
    block(1, 6, True)
    block(1, 2, False)
    forward(3)
    send(5)
    steps(1, 0, 7)
    arrived(2)
    block(2, 5, True)
    block(2, 1, False)
    forward(4)
    send(6)
    steps(1, 0, 3, 6)
    steps(2, 0, 7)
    arrived(3)
    block(3, 4, True)
    block(3, 0, False)
    steps(0, 0, 2, 1)
    forward(5)
    send(7)
    steps(1, 0, 5)
    steps(2, 0, 3, 6)
    steps(3, 0, 7)
    arrived(4)
    block(4, 7, True)
    block(4, 3, False)
    forward(6)
    steps(1, 0, 4)
    steps(2, 0, 5)
    steps(3, 0, -8, 6)
    arrived(5)
    block(5, 6, True)
    block(5, 2, False)
    forward(7)
    steps(1, 0, 2)
    steps(2, 0, 4, -8)
    steps(3, 0, 5, -1)
    arrived(6)
    block(6, 5, True)
    block(6, 1, False)
    arrived(7)
    block(7, 4, True)
    block(7, 0, False)
    steps(0, 1, 3, 2, 1)
    steps(1, 0, -8)
    steps(1, 1, 7, 6, 5)
    steps(2, 0, -1)
    steps(2, 1, 7)
    steps(3, 0, 4, -2)

    def part_copy(r, s, dx, owner):
        there, device = at_x(dx)
        slot = there if owner else x
        return pltpu.make_async_remote_copy(
            src_ref=total.at[r, s, there],
            dst_ref=parts.at[r, s, slot],
            send_sem=part_s.at[r, s, there],
            recv_sem=part_r.at[r, s, slot],
            device_id=device,
            device_id_type=MESH,
        )

    def far_copies(r, s):
        return [
            pltpu.make_async_remote_copy(
                src_ref=here.at[r, s],
                dst_ref=there.at[r, s],
                send_sem=far_s.at[kind, r, s],
                recv_sem=far_r.at[kind, r, s],
                device_id=at_z(8),
                device_id_type=MESH,
            )
            for kind, (here, there) in enumerate(((tops, far_tops), (bottoms, far_bottoms)))
        ]

    def out_copy(r, s, dx, owner):
        there, device = at_x(dx)
        slot = there if owner else x
        return pltpu.make_async_remote_copy(
            src_ref=merged.at[r, s, slot],
            dst_ref=merged.at[r, s, slot],
            send_sem=out_s.at[r, s, there],
            recv_sem=out_r.at[r, s, slot],
            device_id=device,
            device_id_type=MESH,
        )

    def finish(r, s):
        base = s * piece
        own = r * 8 + z
        coded_copy(1 - main, own, s).wait_recv()

        @pl.when(place == 0)
        def _():
            for q in range(4):
                span = slice(base + q * band, base + (q + 1) * band)
                total[r, s, q] = fisher[own, span] * scale + OFFSET + decode(coded[1 - main, own, span])

        @pl.when(place > 0)
        def _():
            coded_copy(main, own, s).wait_recv()
            for q in range(4):
                span = slice(base + q * band, base + (q + 1) * band)
                total[r, s, q] = (
                    fisher[own, span] * scale + decode(coded[main, own, span]) + decode(coded[1 - main, own, span])
                )

        for dx in (1, 2, 3):
            part_copy(r, s, dx, False).start()
        parts[r, s, x] = total[r, s, x]

    def weigh(r, s):
        for dx in (1, 2, 3):
            part_copy(r, s, dx, True).wait_recv()
        damped = [parts[r, s, m] for m in range(4)]
        product = [damped[m] * wparts[m, s, :, r * part:(r + 1) * part] for m in range(4)]
        tops[r, s] = (product[0] + product[1]) + (product[2] + product[3])
        bottoms[r, s] = encode(((damped[0] + damped[1]) + (damped[2] + damped[3])) * 0.25)
        for copy in far_copies(r, s):
            copy.start()

    def merge(r, s):
        for copy in far_copies(r, s):
            copy.wait_recv()
        bottom = decode(bottoms[r, s]) + decode(far_bottoms[r, s])
        merged[r, s, x] = (tops[r, s] + far_tops[r, s]) * 0.25 / bottom
        for dx in (1, 2, 3):
            out_copy(r, s, dx, False).start()

    for s in range(SUBS):
        finish(0, s)
    steps(1, 1, 4)
    steps(2, 1, 6)
    for dx in (1, 2, 3):
        w_copy(dx, True).wait_recv()
    for s in range(SUBS):
        weigh(0, s)
    steps(1, 1, 3, 2, -8)
    steps(2, 1, 5, 4, 3, -8, -1)
    steps(3, 1, 7, 6, -8, 5, -1, 4, -2)
    for s in range(SUBS):
        finish(1, s)
    for s in range(SUBS):
        weigh(1, s)
    for r in range(ROUNDS):
        for s in range(SUBS):
            merge(r, s)
    for r in range(ROUNDS):
        for s in range(SUBS):
            for dx in (1, 2, 3):
                out_copy(r, s, dx, True).wait_recv()
        out_ref[:, :, :, r * part:(r + 1) * part] = merged[r]

    for dy, dc in ((1, 0), (3, 0), (2, 0), (0, 1)):
        row_copy(dy, dc, False).wait_send()
    for dy in (1, 3, 2):
        row_pass(dy, False).wait_send()

    @pl.loop(0, 4 * ROUNDS)
    def _(k):
        for dy, dc in ((1, 0), (3, 0), (1, 1), (3, 1), (0, 1)):
            col_copy(k, dy, dc).wait_send()
        for core in (0, 1):
            col_pass(k, core).wait_send()

    for dx in (1, 2, 3):
        w_copy(dx, False).wait_send()
        for r in range(ROUNDS):
            for s in range(SUBS):
                part_copy(r, s, dx, False).wait_send()
                out_copy(r, s, dx, False).wait_send()
    for r in range(ROUNDS):
        for s in range(SUBS):
            for copy in far_copies(r, s):
                copy.wait_send()

    @pl.loop(0, 8)
    def _(away):
        @pl.when(away != place)
        def _():
            for r in range(ROUNDS):
                for s in range(SUBS):
                    coded_copy(jnp.where(away > place, main, 1 - main), r * 8 + flip(away), s).wait_send()


def shards(inputs, cotangent, token_ids, weights):
    seq, feature = inputs.shape[2:]
    query = cotangent.shape[3]
    height, width = weights.shape[2:]
    band = height // SUBS // 4
    part = width // ROUNDS
    blocks = weights[0, 0].reshape(SUBS, 4, band, width)
    vmem = pl.BlockSpec(memory_space=pltpu.VMEM)
    dma = pltpu.SemaphoreType.DMA
    merged = pl.pallas_call(
        kernel,
        out_shape=jax.ShapeDtypeStruct((SUBS, 4, band, width), jnp.float32),
        in_specs=[pl.BlockSpec(memory_space=pl.ANY)] * 3 + [vmem],
        out_specs=vmem,
        scratch_shapes=[
            pltpu.VMEM((seq, feature), jnp.bfloat16),
            pltpu.VMEM((feature, seq), jnp.bfloat16),
            pltpu.VMEM((seq, query), jnp.bfloat16),
            pltpu.VMEM((SUBS, 4, band, width), jnp.float32),
            pltpu.VMEM((8, 2 * height, seq), jnp.bfloat16),
            pltpu.VMEM((8, 4 * ROUNDS, seq, part), jnp.bfloat16),
            pltpu.VMEM((8 * ROUNDS, height, part), jnp.float32),
            pltpu.VMEM((2, 8 * ROUNDS, height, part), jnp.bfloat16),
            pltpu.VMEM((ROUNDS, SUBS, 4, band, part), jnp.float32),
            pltpu.VMEM((ROUNDS, SUBS, 4, band, part), jnp.float32),
            pltpu.VMEM((4, SUBS, band, width), jnp.float32),
            pltpu.VMEM((ROUNDS, SUBS, band, part), jnp.float32),
            pltpu.VMEM((ROUNDS, SUBS, band, part), jnp.bfloat16),
            pltpu.VMEM((ROUNDS, SUBS, band, part), jnp.float32),
            pltpu.VMEM((ROUNDS, SUBS, band, part), jnp.bfloat16),
            pltpu.VMEM((ROUNDS, SUBS, 4, band, part), jnp.float32),
            dma((3,)),
            dma((8,)), dma((8,)), dma((4 * ROUNDS, 8)), dma((4 * ROUNDS, 8)),
            dma((2, 8 * ROUNDS, SUBS)), dma((2, 8 * ROUNDS, SUBS)),
            dma((4,)), dma((4,)), dma((ROUNDS, SUBS, 4)), dma((ROUNDS, SUBS, 4)),
            dma((2, ROUNDS, SUBS)), dma((2, ROUNDS, SUBS)), dma((ROUNDS, SUBS, 4)), dma((ROUNDS, SUBS, 4)),
        ],
        compiler_params=pltpu.CompilerParams(collective_id=0, has_side_effects=True),
    )(inputs[0, 0], cotangent[0, 0], blocks, token_ids[0])
    return merged.reshape(1, height, width)


def solution(mesh):
    in_specs = (
        P("mp", "tok", None, None),
        P("mp", "tok", None, None),
        P("mp", "tok", None),
        P("mp", "tok", None, None),
    )
    out_specs = P("tok", None, None)
    return jax.shard_map(shards, mesh=mesh, in_specs=in_specs, out_specs=out_specs, check_vma=False)
```

time: 123 us -> 118 us (0.959)
  the two profiles are of different devices: /device:TPU:120 before, /device:TPU:8 now
where the time goes in v4:
time: 118 us
  Pallas kernels  116 us (98%)
  local copies, waits for them, and re-layouts  1.87 us (2%)
    pallas_call x1, Pallas kernels, shards(): pl.pallas_call(kernel, out_shape=jax.ShapeDtypeStruct((SUBS, 4, band, wid...  116 us

profile of v4, /device:TPU:8, one launch (start us, length us, event | category | flops | bytes accessed | tf_op | source)
XLA Modules:
  0.0 118.1 jit_solution(715684877122836151)
XLA Ops:
  0.0 116.2 %shard_map.46 = f32[2,4,32,512]{3,2,1,0:T(8,128)} custom-call(bf16[128,2048]{1,0:T(8,128)(2,1)} %bitcast.7, bf16[128,4096]{1,0:T(8,128)(2,1)} %bitcast.6, f32[2,4,32,512]{3,2,1,0:T(8,128)} %bitcast.8, s32[1,128]{1,0:T(1,128)} %bitcast.9), custom_call_target="tpu_custom_call" | custom-call | tf_op jit(solution)/shard_map/pallas_call | solution.py:473
  116.2 1.9 %copy.6 = f32[1,256,512]{2,1,0:T(8,128)} copy(f32[1,256,512]{2,1,0:T(8,128)} %bitcast.5) | data formatting | bytes 1048576

commit v5 on v4

v5 whole, which is shorter than its diff:
```python
import jax
import jax.numpy as jnp
from jax import lax
from jax.experimental import pallas as pl
from jax.experimental.pallas import tpu as pltpu
from jax.sharding import PartitionSpec as P

FIRST_TEXT = 37984
DAMPING = 0.1
WIDTHS = (256, 256)
ROUNDS = len(WIDTHS)
STARTS = tuple(sum(WIDTHS[:r]) for r in range(ROUNDS))
SUBS = 4
HALVES = 2
MESH = pl.DeviceIdType.MESH
Y_PEERS = ((1, 0), (3, 0), (1, 1), (3, 1), (2, 0), (2, 1), (0, 1))
OFFSET = DAMPING / 2
MIDDLE = 90.5
LOW_UNIT = 2.0
HIGH_UNIT = 4096.0


def encode(values):
    small = values < MIDDLE
    ratio = values * jnp.where(small, 1.0 / LOW_UNIT, 1.0 / HIGH_UNIT)
    square = ratio * ratio
    fourth = square * square
    eighth = fourth * fourth
    power = (eighth * eighth) * (fourth * square)
    return jnp.where(small, power, -power).astype(jnp.bfloat16)


def decode(code):
    power = code.astype(jnp.float32)
    ratio = jnp.exp2(jnp.log2(jnp.abs(power)) * (1.0 / 22))
    return ratio * jnp.where(power > 0, LOW_UNIT, HIGH_UNIT)


def kernel(
    x_hbm, g_hbm, w_hbm, ids_ref, out_ref,
    x_ref, xt_ref, g_ref, w_ref, rows, cols, fisher, coded, total, parts, wparts,
    tops, bottoms, far_tops, far_bottoms, merged, load_s,
    row_s, row_r, col_s, col_r, coded_s, coded_r,
    w_s, w_r, part_s, part_r, far_s, far_r, out_s, out_r,
):
    loads = (
        pltpu.make_async_copy(x_hbm, x_ref, load_s.at[0]),
        pltpu.make_async_copy(g_hbm, g_ref, load_s.at[1]),
        pltpu.make_async_copy(w_hbm, w_ref, load_s.at[2]),
    )
    for load in (loads[1], loads[0], loads[2]):
        load.start()
    mp = lax.axis_index("mp")
    tok = lax.axis_index("tok")
    x, zh = mp // 2, mp % 2
    y, z, c = tok // 16, (tok // 2) % 8, tok % 2
    me = y * 2 + c
    seq = g_ref.shape[0]
    width = w_ref.shape[3]
    height = w_ref.shape[0] * w_ref.shape[1] * w_ref.shape[2]
    piece = height // SUBS
    band = height // HALVES // 4

    def at_y(dy, dc):
        there = (y + dy) % 4
        core = 1 - c if dc else c
        return there, core, (mp, (there * 8 + z) * 2 + core)

    def at_x(dx):
        there = (x + dx) % 4
        return there, (there * 2 + zh, tok)

    def at_z(dz):
        deep = zh * 8 + z + dz + 16
        return (x * 2 + (deep // 8) % 2, (y * 8 + deep % 8) * 2 + c)

    barrier = pltpu.get_barrier_semaphore()
    for dy, dc in Y_PEERS:
        pl.semaphore_signal(barrier, 1, device_id=at_y(dy, dc)[2], device_id_type=MESH)
    for dx in (1, 2, 3):
        pl.semaphore_signal(barrier, 1, device_id=at_x(dx)[1], device_id_type=MESH)
    for dz in (1, -1, 8):
        pl.semaphore_signal(barrier, 1, device_id=at_z(dz), device_id_type=MESH)
    pl.semaphore_wait(barrier, len(Y_PEERS) + 6)

    loads[1].wait()

    low = z < 4

    def unit_of(u):
        return u // 4, jnp.where(low, 3 - u % 4, u % 4)

    def columns(r, k, core):
        return pl.ds(pl.multiple_of((2 * k + core) * width + STARTS[r], 128), WIDTHS[r])

    def row_copy(dy, dc, owner):
        there, core, device = at_y(dy, dc)
        slot = there * 2 + core if owner else me
        return pltpu.make_async_remote_copy(
            src_ref=xt_ref.at[pl.ds(there * 2 * height, 2 * height)],
            dst_ref=rows.at[slot],
            send_sem=row_s.at[there * 2 + core],
            recv_sem=row_r.at[slot],
            device_id=device,
            device_id_type=MESH,
        )

    def row_pass(dy, owner):
        there = (y + dy) % 4
        slot = there * 2 + (1 - c if owner else c)
        return pltpu.make_async_remote_copy(
            src_ref=rows.at[slot],
            dst_ref=rows.at[slot],
            send_sem=row_s.at[there * 2 + 1 - c],
            recv_sem=row_r.at[slot],
            device_id=at_y(0, 1)[2],
            device_id_type=MESH,
        )

    def col_copy(r, k, dy, dc):
        there, core, device = at_y(dy, dc)
        return pltpu.make_async_remote_copy(
            src_ref=g_ref.at[:, columns(r, k, core)],
            dst_ref=cols[r].at[me, k],
            send_sem=col_s.at[r, k, there * 2 + core],
            recv_sem=col_r.at[r, k, me],
            device_id=device,
            device_id_type=MESH,
        )

    def col_wait(r, k, slot):
        pltpu.make_async_remote_copy(
            src_ref=cols[r].at[slot, k],
            dst_ref=cols[r].at[slot, k],
            send_sem=col_s.at[r, k, slot],
            recv_sem=col_r.at[r, k, slot],
            device_id=at_y(0, 1)[2],
            device_id_type=MESH,
        ).wait_recv()

    def col_pass(r, k, core):
        step = 1 - 2 * core
        slot = ((y + 4 - step) % 4) * 2 + core
        return pltpu.make_async_remote_copy(
            src_ref=cols[r].at[slot, k],
            dst_ref=cols[r].at[slot, k],
            send_sem=col_s.at[r, k, ((y + 2) % 4) * 2 + core],
            recv_sem=col_r.at[r, k, slot],
            device_id=at_y(step + 4, 0)[2],
            device_id_type=MESH,
        )

    def w_copy(dx, owner):
        there, device = at_x(dx)
        slot = there if owner else x
        return pltpu.make_async_remote_copy(
            src_ref=w_ref.at[:, there],
            dst_ref=wparts.at[slot],
            send_sem=w_s.at[there],
            recv_sem=w_r.at[slot],
            device_id=device,
            device_id_type=MESH,
        )

    def send(u):
        for dy, dc in ((1, 0), (3, 0), (1, 1), (3, 1), (0, 1)):
            col_copy(*unit_of(u), dy, dc).start()

    def forward(u):
        for core in (0, 1):
            slot = ((y + 3 + 2 * core) % 4) * 2 + core
            col_wait(*unit_of(u), slot)
            col_pass(*unit_of(u), core).start()

    send(0)

    loads[0].wait()
    kept = ids_ref[...] >= FIRST_TEXT
    for r in range(8):
        some = x_ref[:, r * height:(r + 1) * height].astype(jnp.float32).T
        xt_ref[r * height:(r + 1) * height, :] = jnp.where(kept, some, 0.0).astype(jnp.bfloat16)

    for dy, dc in ((1, 0), (3, 0), (2, 0), (0, 1)):
        row_copy(dy, dc, False).start()
    send(1)
    loads[2].wait()
    for dx in (1, 2, 3):
        w_copy(dx, False).start()

    rows[me] = xt_ref[pl.ds(y * 2 * height, 2 * height), :]
    for r in range(ROUNDS):
        for k in range(4):
            cols[r][me, k] = g_ref[:, columns(r, k, c)]
    wparts[x] = w_ref[:, x]

    forward(0)
    for dy in (1, 3, 2):
        row_copy(dy, 0, True).wait_recv()
        row_pass(dy, False).start()
    send(2)
    row_copy(0, 1, True).wait_recv()
    for dy in (1, 3, 2):
        row_pass(dy, True).wait_recv()

    def arrived(u):
        r, k = unit_of(u)
        for slot in (((y + 3) % 4) * 2 + 1, ((y + 1) % 4) * 2, y * 2 + 1 - c, ((y + 2) % 4) * 2, ((y + 2) % 4) * 2 + 1):
            col_wait(r, k, slot)

    scale = 1.0 / (seq * 64)
    main = jnp.where(low, 0, 1)
    place = jnp.where(low, z, 7 - z)

    def flip(d):
        return jnp.where(low, d, 7 - d)

    def coded_copy(way, r, d, s):
        span = pl.ds(s * piece, piece)
        return pltpu.make_async_remote_copy(
            src_ref=coded[r].at[way, d, span],
            dst_ref=coded[r].at[way, d, span],
            send_sem=coded_s.at[way, r, d],
            recv_sem=coded_r.at[way, r, d, s],
            device_id=at_z(1 - 2 * way),
            device_id_type=MESH,
        )

    def coded_sent(way, r, d):
        pltpu.make_async_remote_copy(
            src_ref=coded[r].at[way, d],
            dst_ref=coded[r].at[way, d],
            send_sem=coded_s.at[way, r, d],
            recv_sem=coded_r.at[way, r, d, 0],
            device_id=at_z(1 - 2 * way),
            device_id_type=MESH,
        ).wait_send()

    def piece_of(s):
        return pl.ds(pl.multiple_of(s * piece, piece), piece)

    def first_step(r, away):
        d = flip(away)

        @pl.loop(0, SUBS)
        def _(s):
            coded[r][main, d, piece_of(s)] = encode(fisher[r][d, piece_of(s)] * scale + OFFSET)
            coded_copy(main, r, d, s).start()

    def step(way, r, away):
        d = flip(away)

        @pl.loop(0, SUBS)
        def _(s):
            coded_copy(way, r, d, s).wait_recv()
            own = fisher[r][d, piece_of(s)] * scale
            coded[r][way, d, piece_of(s)] = encode(decode(coded[r][way, d, piece_of(s)]) + own)
            coded_copy(way, r, d, s).start()

    def block(u, away, early):
        r, k = unit_of(u)
        d = flip(away)
        base = d // 4 * height

        @pl.loop(0, SUBS)
        def _(s):
            summed = None
            for slot in range(8):
                left = rows[slot, pl.ds(pl.multiple_of(base + s * piece, piece), piece), :]
                gradient = jnp.dot(left, cols[r][slot, k], preferred_element_type=jnp.float32)
                square = gradient * gradient
                summed = square if summed is None else summed + square
            fisher[r][d, piece_of(s)] = summed
            if early:
                @pl.when(place == 0)
                def _():
                    coded[r][main, d, piece_of(s)] = encode(summed * scale + OFFSET)
                    coded_copy(main, r, d, s).start()

    def steps(where, r, *aways):
        @pl.when(place == where)
        def _():
            for away in aways:
                if where == 0:
                    first_step(r, away)
                elif away < 0:
                    step(1 - main, r, -away % 8)
                else:
                    step(main, r, away)

    forward(1)
    send(3)
    arrived(0)
    block(0, 7, True)
    block(0, 3, True)
    forward(2)
    send(4)
    arrived(1)
    block(1, 6, True)
    block(1, 2, False)
    forward(3)
    send(5)
    steps(1, 0, 7)
    arrived(2)
    block(2, 5, True)
    block(2, 1, False)
    forward(4)
    send(6)
    steps(1, 0, 3, 6)
    steps(2, 0, 7)
    arrived(3)
    block(3, 4, True)
    block(3, 0, False)
    steps(0, 0, 2, 1)
    forward(5)
    send(7)
    steps(1, 0, 5)
    steps(2, 0, 3, 6)
    steps(3, 0, 7)
    arrived(4)
    block(4, 7, True)
    block(4, 3, False)
    forward(6)
    steps(1, 0, 4)
    steps(2, 0, 5)
    steps(3, 0, -8, 6)
    arrived(5)
    block(5, 6, True)
    block(5, 2, False)
    forward(7)
    steps(1, 0, 2)
    steps(2, 0, 4, -8)
    steps(3, 0, 5, -1)
    arrived(6)
    block(6, 5, True)
    block(6, 1, False)
    arrived(7)
    block(7, 4, True)
    block(7, 0, False)
    steps(0, 1, 3, 2, 1)
    steps(1, 0, -8)
    steps(1, 1, 7, 6, 5)
    steps(2, 0, -1)
    steps(2, 1, 7)
    steps(3, 0, 4, -2)

    def part_copy(r, s, dx, owner):
        there, device = at_x(dx)
        slot = there if owner else x
        return pltpu.make_async_remote_copy(
            src_ref=total[r].at[s, there],
            dst_ref=parts[r].at[s, slot],
            send_sem=part_s.at[r, s, there],
            recv_sem=part_r.at[r, s, slot],
            device_id=device,
            device_id_type=MESH,
        )

    def far_copies(r, s):
        return [
            pltpu.make_async_remote_copy(
                src_ref=here[r].at[s],
                dst_ref=there[r].at[s],
                send_sem=far_s.at[kind, r, s],
                recv_sem=far_r.at[kind, r, s],
                device_id=at_z(8),
                device_id_type=MESH,
            )
            for kind, (here, there) in enumerate(((tops, far_tops), (bottoms, far_bottoms)))
        ]

    def out_copy(r, s, dx, owner):
        there, device = at_x(dx)
        slot = there if owner else x
        return pltpu.make_async_remote_copy(
            src_ref=merged[r].at[s, slot],
            dst_ref=merged[r].at[s, slot],
            send_sem=out_s.at[r, s, there],
            recv_sem=out_r.at[r, s, slot],
            device_id=device,
            device_id_type=MESH,
        )

    def finish(r, s):
        base = s * 4 * band
        inner = range(s * SUBS // HALVES, (s + 1) * SUBS // HALVES)
        for one in inner:
            coded_copy(1 - main, r, z, one).wait_recv()

        @pl.when(place == 0)
        def _():
            for q in range(4):
                span = slice(base + q * band, base + (q + 1) * band)
                total[r][s, q] = fisher[r][z, span] * scale + OFFSET + decode(coded[r][1 - main, z, span])

        @pl.when(place > 0)
        def _():
            for one in inner:
                coded_copy(main, r, z, one).wait_recv()
            for q in range(4):
                span = slice(base + q * band, base + (q + 1) * band)
                total[r][s, q] = (
                    fisher[r][z, span] * scale + decode(coded[r][main, z, span]) + decode(coded[r][1 - main, z, span])
                )

        for dx in (1, 2, 3):
            part_copy(r, s, dx, False).start()
        parts[r][s, x] = total[r][s, x]

    def weigh(r, s):
        for dx in (1, 2, 3):
            part_copy(r, s, dx, True).wait_recv()
        damped = [parts[r][s, m] for m in range(4)]
        product = [damped[m] * wparts[m, s, :, STARTS[r]:STARTS[r] + WIDTHS[r]] for m in range(4)]
        tops[r][s] = (product[0] + product[1]) + (product[2] + product[3])
        bottoms[r][s] = encode(((damped[0] + damped[1]) + (damped[2] + damped[3])) * 0.25)
        for copy in far_copies(r, s):
            copy.start()

    def merge(r, s):
        for copy in far_copies(r, s):
            copy.wait_recv()
        bottom = decode(bottoms[r][s]) + decode(far_bottoms[r][s])
        merged[r][s, x] = (tops[r][s] + far_tops[r][s]) * 0.25 / bottom
        for dx in (1, 2, 3):
            out_copy(r, s, dx, False).start()

    for s in range(HALVES):
        finish(0, s)
    steps(1, 1, 4)
    steps(2, 1, 6)
    for dx in (1, 2, 3):
        w_copy(dx, True).wait_recv()
    for s in range(HALVES):
        weigh(0, s)
    steps(1, 1, 3, 2, -8)
    steps(2, 1, 5, 4, 3, -8, -1)
    steps(3, 1, 7, 6, -8, 5, -1, 4, -2)
    for s in range(HALVES):
        finish(1, s)
    for s in range(HALVES):
        weigh(1, s)
    for r in range(ROUNDS):
        for s in range(HALVES):
            merge(r, s)
    for r in range(ROUNDS):
        for s in range(HALVES):
            for dx in (1, 2, 3):
                out_copy(r, s, dx, True).wait_recv()
        out_ref[:, :, :, STARTS[r]:STARTS[r] + WIDTHS[r]] = merged[r][...]

    for dy, dc in ((1, 0), (3, 0), (2, 0), (0, 1)):
        row_copy(dy, dc, False).wait_send()
    for dy in (1, 3, 2):
        row_pass(dy, False).wait_send()

    @pl.loop(0, 4)
    def _(k):
        for r in range(ROUNDS):
            for dy, dc in ((1, 0), (3, 0), (1, 1), (3, 1), (0, 1)):
                col_copy(r, k, dy, dc).wait_send()
            for core in (0, 1):
                col_pass(r, k, core).wait_send()

    for dx in (1, 2, 3):
        w_copy(dx, False).wait_send()
        for r in range(ROUNDS):
            for s in range(HALVES):
                part_copy(r, s, dx, False).wait_send()
                out_copy(r, s, dx, False).wait_send()
    for r in range(ROUNDS):
        for s in range(HALVES):
            for copy in far_copies(r, s):
                copy.wait_send()

    @pl.loop(0, 8)
    def _(away):
        @pl.when(away != place)
        def _():
            for r in range(ROUNDS):
                coded_sent(jnp.where(away > place, main, 1 - main), r, flip(away))


def shards(inputs, cotangent, token_ids, weights):
    seq, feature = inputs.shape[2:]
    query = cotangent.shape[3]
    height, width = weights.shape[2:]
    band = height // HALVES // 4
    blocks = weights[0, 0].reshape(HALVES, 4, band, width)
    vmem = pl.BlockSpec(memory_space=pltpu.VMEM)
    dma = pltpu.SemaphoreType.DMA
    merged = pl.pallas_call(
        kernel,
        out_shape=jax.ShapeDtypeStruct((HALVES, 4, band, width), jnp.float32),
        in_specs=[pl.BlockSpec(memory_space=pl.ANY)] * 3 + [vmem],
        out_specs=vmem,
        scratch_shapes=[
            pltpu.VMEM((seq, feature), jnp.bfloat16),
            pltpu.VMEM((feature, seq), jnp.bfloat16),
            pltpu.VMEM((seq, query), jnp.bfloat16),
            pltpu.VMEM((HALVES, 4, band, width), jnp.float32),
            pltpu.VMEM((8, 2 * height, seq), jnp.bfloat16),
            [pltpu.VMEM((8, 4, seq, part), jnp.bfloat16) for part in WIDTHS],
            [pltpu.VMEM((8, height, part), jnp.float32) for part in WIDTHS],
            [pltpu.VMEM((2, 8, height, part), jnp.bfloat16) for part in WIDTHS],
            [pltpu.VMEM((HALVES, 4, band, part), jnp.float32) for part in WIDTHS],
            [pltpu.VMEM((HALVES, 4, band, part), jnp.float32) for part in WIDTHS],
            pltpu.VMEM((4, HALVES, band, width), jnp.float32),
            [pltpu.VMEM((HALVES, band, part), jnp.float32) for part in WIDTHS],
            [pltpu.VMEM((HALVES, band, part), jnp.bfloat16) for part in WIDTHS],
            [pltpu.VMEM((HALVES, band, part), jnp.float32) for part in WIDTHS],
            [pltpu.VMEM((HALVES, band, part), jnp.bfloat16) for part in WIDTHS],
            [pltpu.VMEM((HALVES, 4, band, part), jnp.float32) for part in WIDTHS],
            dma((3,)),
            dma((8,)), dma((8,)), dma((ROUNDS, 4, 8)), dma((ROUNDS, 4, 8)),
            dma((2, ROUNDS, 8)), dma((2, ROUNDS, 8, SUBS)),
            dma((4,)), dma((4,)), dma((ROUNDS, HALVES, 4)), dma((ROUNDS, HALVES, 4)),
            dma((2, ROUNDS, HALVES)), dma((2, ROUNDS, HALVES)), dma((ROUNDS, HALVES, 4)), dma((ROUNDS, HALVES, 4)),
        ],
        compiler_params=pltpu.CompilerParams(collective_id=0, has_side_effects=True),
    )(inputs[0, 0], cotangent[0, 0], blocks, token_ids[0])
    return merged.reshape(1, height, width)


def solution(mesh):
    in_specs = (
        P("mp", "tok", None, None),
        P("mp", "tok", None, None),
        P("mp", "tok", None),
        P("mp", "tok", None, None),
    )
    out_specs = P("tok", None, None)
    return jax.shard_map(shards, mesh=mesh, in_specs=in_specs, out_specs=out_specs, check_vma=False)
```

time: 118 us -> 115 us (0.975)
  the two profiles are of different devices: /device:TPU:8 before, /device:TPU:16 now
where the time goes in v5:
time: 115 us
  Pallas kernels  113 us (98%)
  local copies, waits for them, and re-layouts  1.87 us (2%)
    pallas_call x1, Pallas kernels, shards(): pl.pallas_call(kernel, out_shape=jax.ShapeDtypeStruct((HALVES, 4, band, w...  113 us

profile of v5, /device:TPU:16, one launch (start us, length us, event | category | flops | bytes accessed | tf_op | source)
XLA Modules:
  0.0 115.3 jit_solution(10634326988080739543)
XLA Ops:
  0.0 113.4 %shard_map.46 = f32[2,4,32,512]{3,2,1,0:T(8,128)} custom-call(bf16[128,2048]{1,0:T(8,128)(2,1)} %bitcast.7, bf16[128,4096]{1,0:T(8,128)(2,1)} %bitcast.6, f32[2,4,32,512]{3,2,1,0:T(8,128)} %bitcast.8, s32[1,128]{1,0:T(1,128)} %bitcast.9), custom_call_target="tpu_custom_call" | custom-call | tf_op jit(solution)/shard_map/pallas_call | solution.py:491
  113.4 1.9 %copy.6 = f32[1,256,512]{2,1,0:T(8,128)} copy(f32[1,256,512]{2,1,0:T(8,128)} %bitcast.5) | data formatting | bytes 1048576

commit v6 on v5

--- a/solution.py
+++ b/solution.py
@@ -163,8 +163,10 @@
         )
 
     def send(u):
-        for dy, dc in ((1, 0), (3, 0), (1, 1), (3, 1), (0, 1)):
-            col_copy(*unit_of(u), dy, dc).start()
+        for dy in (1 + 2 * c, 3 - 2 * c):
+            for dc in (0, 1):
+                col_copy(*unit_of(u), dy, dc).start()
+        col_copy(*unit_of(u), 0, 1).start()
 
     def forward(u):
         for core in (0, 1):

time: 115 us -> 115 us (level)
  no operation moved by 1% of the time
where the time goes in v6:
time: 115 us
  Pallas kernels  113 us (98%)
  local copies, waits for them, and re-layouts  1.87 us (2%)
    pallas_call x1, Pallas kernels, shards(): pl.pallas_call(kernel, out_shape=jax.ShapeDtypeStruct((HALVES, 4, band, w...  113 us

profile of v6, /device:TPU:16, one launch (start us, length us, event | category | flops | bytes accessed | tf_op | source)
XLA Modules:
  0.0 115.3 jit_solution(11094871109807149885)
XLA Ops:
  0.0 113.4 %shard_map.46 = f32[2,4,32,512]{3,2,1,0:T(8,128)} custom-call(bf16[128,2048]{1,0:T(8,128)(2,1)} %bitcast.7, bf16[128,4096]{1,0:T(8,128)(2,1)} %bitcast.6, f32[2,4,32,512]{3,2,1,0:T(8,128)} %bitcast.8, s32[1,128]{1,0:T(1,128)} %bitcast.9), custom_call_target="tpu_custom_call" | custom-call | tf_op jit(solution)/shard_map/pallas_call | solution.py:493
  113.5 1.9 %copy.6 = f32[1,256,512]{2,1,0:T(8,128)} copy(f32[1,256,512]{2,1,0:T(8,128)} %bitcast.5) | data formatting | bytes 1048576
